TPU v7x, 256 devices: a whole 4x4x8 slice. The times are simulated.
256 devices in a mesh: gx: 8 (over y, core), gy: 4 (over x), gz: 8 (over z).
Axes of the slice: x: 4, y: 4, z: 8, core: 2. Of those that a mesh axis runs over, the one named last changes fastest.
Arguments:
- positions: float32 [3, 32, 16, 1024], P(None, 'gx', 'gy', 'gz'), may hold values from 0 to 1
- charges: float32 [32, 16, 1024], P('gx', 'gy', 'gz'), may hold values from -1.2 to 1.2
- counts: int32 [32, 16, 32], P('gx', 'gy', 'gz'), may hold values from 16 to 32
- moment_shift: bfloat16 [8, 81, 81], replicated, may hold values from -0.25 to 0.25
- far_operators: bfloat16 [81, 25600], replicated, may hold values from -0.046875 to 0.046875
- local_shift: bfloat16 [8, 81, 81], replicated, may hold values from -0.625 to 0.625
- lattice_operator: bfloat16 [81, 81], replicated, may hold values from -0.625 to 0.625
Outputs:
- potential: float32 [32, 16, 1024], P('gx', 'gy', 'gz')
- electric_field: float32 [3, 32, 16, 1024], P(None, 'gx', 'gy', 'gz')
Inputs may be any that keep to these rules, and one draw needn't show every extreme that they name: `counts`: number of live charges in each leaf; slots at or past it are pads.
All inputs are finite; a program needn't handle non-finite values.
Results may differ from a plain program's by a relative error of at most 0.00035.
Values sent between devices are 32-bit elements; how exact they have to be, the bound alone decides.
A program may use at most 256 MiB of HBM per device.

v0:
```python
import functools

import jax
import jax.numpy as jnp
import numpy as np
from jax import lax
from jax.experimental import pallas as pl
from jax.experimental.pallas import tpu as pltpu
from jax.sharding import PartitionSpec as P

ORDER = 8
SLOTS = 32
SOFTENING = 0.0625
TERMS = 81
KPAD = 96
LANES = 128
OFFSETS = 316
CHUNK = 8
MESH = pl.DeviceIdType.MESH
F32 = jnp.float32
BF16 = jnp.bfloat16


def offset_table():
    listed = []
    for shift_x in range(-3, 4):
        for shift_y in range(-3, 4):
            for shift_z in range(-3, 4):
                if max(abs(shift_x), abs(shift_y), abs(shift_z)) >= 2:
                    listed.append((shift_x, shift_y, shift_z))
    return listed


def exponent_list():
    listed = []
    for accumulated in range(ORDER + 1):
        for height in (0, 1):
            for power_x in range(accumulated - height + 1):
                listed.append((power_x, accumulated - height - power_x, height))
    return listed


def exponent_planes():
    planes = np.zeros((4, KPAD, LANES), np.int32)
    for row, (a, b, c) in enumerate(exponent_list()):
        planes[0, row], planes[1, row], planes[2, row], planes[3, row] = a, b, c, 1
    return planes


def slope_matrix():
    listed = exponent_list()
    place = {e: i for i, e in enumerate(listed)}
    matrix = np.zeros((TERMS, 3 * LANES), np.float32)
    for row, (a, b, c) in enumerate(listed):
        if a > 0:
            matrix[row, place[(a - 1, b, c)]] = a
        if b > 0:
            matrix[row, LANES + place[(a, b - 1, c)]] = b
        if c > 0:
            matrix[row, 2 * LANES + place[(a, b, c - 1)]] = c
    return matrix


def lanes_nt(lhs, rhs):
    return lax.dot_general(lhs, rhs, (((1,), (1,)), ((), ())), preferred_element_type=F32)


def halves(value):
    upper = value.astype(BF16)
    return upper, (value - upper.astype(F32)).astype(BF16)


def split_nt(value, rhs):
    rows = value.shape[0]
    if rows % 8:
        value = jnp.concatenate([value, jnp.zeros((8 - rows, value.shape[1]), F32)], axis=0)
    upper, lower = halves(value)
    both = lanes_nt(upper, rhs) + lanes_nt(lower, rhs)
    return both[:rows]


def widen(value):
    return jnp.concatenate([value, jnp.zeros((value.shape[0], LANES - value.shape[1]), F32)], axis=1)


def power_of(base, exponents):
    square = base * base
    fourth = square * square
    eighth = fourth * fourth
    result = jnp.where((exponents & 1) != 0, base, 1.0)
    result = result * jnp.where((exponents & 2) != 0, square, 1.0)
    result = result * jnp.where((exponents & 4) != 0, fourth, 1.0)
    return jnp.where(exponents == 8, eighth, result)


def monomial_tiles(rows_of, exps_ref, high_ref, low_ref):
    for tile in range(16):
        px, py, ox, oy = tile >> 3, tile >> 2 & 1, tile >> 1 & 1, tile & 1
        row_x, row_y, row_z = rows_of(2 * px + ox, 2 * py + oy)
        full = lambda row: jnp.broadcast_to(row - 0.5, (KPAD, LANES))
        value = power_of(full(row_x), exps_ref[0]) * power_of(full(row_y), exps_ref[1])
        value = value * jnp.where(exps_ref[2] != 0, full(row_z), 1.0)
        value = jnp.where(exps_ref[3] != 0, value, 0.0)
        upper, lower = halves(value)
        high_ref[:, tile * LANES : (tile + 1) * LANES] = upper
        low_ref[:, tile * LANES : (tile + 1) * LANES] = lower


def moments_kernel(
    pos_ref, chg_ref, cnt_ref, exps_ref, up_ref, data_ref, live_ref, leaf_ref, mid_ref, top_ref, high_ref, low_ref
):
    counts = jnp.concatenate([cnt_ref[x] for x in range(4)], axis=0).astype(F32).astype(BF16)
    spread = (
        lax.broadcasted_iota(jnp.int32, (4, LANES), 1) // SLOTS == lax.broadcasted_iota(jnp.int32, (4, LANES), 0)
    ).astype(F32).astype(BF16)
    limit = jnp.dot(counts, spread, preferred_element_type=F32)
    slot_of = (lax.broadcasted_iota(jnp.int32, (16, LANES), 1) % SLOTS).astype(F32)
    live = (slot_of < limit).astype(F32)
    for x in range(4):
        live_ref[x] = live[4 * x : 4 * x + 4]
        for y in range(4):
            for c in range(3):
                data_ref[x, y, c : c + 1, :] = pos_ref[c, x, y : y + 1, :]
            data_ref[x, y, 3:4, :] = chg_ref[x, y : y + 1, :] * live[4 * x + y : 4 * x + y + 1]

    def rows_of(x, y):
        return tuple(pos_ref[c, x, y : y + 1, :] for c in range(3))

    monomial_tiles(rows_of, exps_ref, high_ref, low_ref)
    row = lax.broadcasted_iota(jnp.int32, (16, LANES), 0)
    lane = lax.broadcasted_iota(jnp.int32, (16, LANES), 1)
    for group in range(4):
        px, py = group >> 1, group & 1
        pieces = []
        for tile in range(4):
            ox, oy = tile >> 1, tile & 1
            hit = (row // 8 == lane // 64) & (row % 8 == ox * 4 + oy * 2 + lane // 32 % 2)
            weight = jnp.broadcast_to(data_ref[2 * px + ox, 2 * py + oy, 3:4, :], (16, LANES))
            pieces.append(jnp.where(hit, weight, 0.0))
        upper, lower = halves(jnp.concatenate(pieces, axis=1))
        span = slice(group * 512, group * 512 + 512)
        both = lanes_nt(jnp.concatenate([upper, lower], axis=0), high_ref[:, span])
        total = both[:16] + both[16:] + lanes_nt(upper, low_ref[:, span])
        leaf_ref[group * 16 : group * 16 + 16, :] = widen(total)
    mid = jnp.zeros((8, TERMS), F32)
    for octant in range(8):
        mid = mid + split_nt(leaf_ref[pl.ds(octant, 8, stride=8), :][:, :TERMS], up_ref[octant])
    mid_ref[...] = widen(mid)
    which = lax.broadcasted_iota(jnp.int32, (8, TERMS), 0)
    top = jnp.zeros((8, TERMS), F32)
    for octant in range(8):
        top = top + jnp.where(which == octant, split_nt(mid, up_ref[octant]), 0.0)
    top_ref[...] = widen(jnp.sum(top, axis=0, keepdims=True))


DIRECTIONS = [
    (dx, dy, dz) for dx in (-1, 0, 1) for dy in (-1, 0, 1) for dz in (-1, 0, 1) if (dx, dy, dz) != (0, 0, 0)
]


def span_of(step, own, first):
    if step == 0:
        return pl.ds(0, own), pl.ds(first, own)
    if step > 0:
        return pl.ds(own - 1, 1), pl.ds(first - 1, 1)
    return pl.ds(0, 1), pl.ds(first + own, 1)


def exchange_kernel(
    nx, ny, nz, data_ref, leaf_ref, mid_ref, top_ref, ext_ref, wide_ref, mids_ref, tops_ref, send, recv, gsend, grecv, own
):
    ix, iy, iz = lax.axis_index("gx"), lax.axis_index("gy"), lax.axis_index("gz")

    def at(dx, dy, dz):
        return {
            "gx": lax.rem(ix + (dx + nx), nx),
            "gy": lax.rem(iy + (dy + ny), ny),
            "gz": lax.rem(iz + (dz + nz), nz),
        }

    partners = list(DIRECTIONS)
    partners += [(0, 0, k) for k in range(2, nz - 1)]
    partners += [(0, k, 0) for k in range(2, ny - 1)]
    partners += [(k, 0, 0) for k in range(2, nx - 1)]
    barrier = pltpu.get_barrier_semaphore()
    for step in partners:
        pl.semaphore_signal(barrier, inc=1, device_id=at(*step), device_id_type=MESH)
    pl.semaphore_wait(barrier, len(partners))

    def remote(src, dst, ssem, rsem, step):
        copy = pltpu.make_async_remote_copy(
            src_ref=src, dst_ref=dst, send_sem=ssem, recv_sem=rsem, device_id=at(*step), device_id_type=MESH
        )
        copy.start()
        return copy

    first = [
        remote(top_ref, tops_ref.at[ix, iy, iz], gsend.at[k], grecv.at[k], (0, 0, k)) for k in range(1, nz)
    ]
    local = [
        pltpu.make_async_copy(top_ref, tops_ref.at[ix, iy, iz], own.at[0]),
        pltpu.make_async_copy(mid_ref, mids_ref.at[13], own.at[1]),
        pltpu.make_async_copy(leaf_ref, wide_ref.at[pl.ds(1, 2), pl.ds(1, 2), pl.ds(1, 2)], own.at[2]),
        pltpu.make_async_copy(data_ref, ext_ref.at[pl.ds(1, 4), pl.ds(1, 4), 1], own.at[3]),
    ]
    for copy in local:
        copy.start()
    copies = []
    for index, step in enumerate(DIRECTIONS):
        dx, dy, dz = step
        from_x, to_x = span_of(dx, 4, 1)
        from_y, to_y = span_of(dy, 4, 1)
        copies.append(
            remote(
                data_ref.at[from_x, from_y],
                ext_ref.at[to_x, to_y, 1 - dz],
                send.at[0, index],
                recv.at[0, index],
                step,
            )
        )
    for index, step in enumerate(DIRECTIONS):
        dx, dy, dz = step
        from_x, to_x = span_of(dx, 2, 1)
        from_y, to_y = span_of(dy, 2, 1)
        from_z, to_z = span_of(dz, 2, 1)
        copies.append(
            remote(
                leaf_ref.at[from_x, from_y, from_z],
                wide_ref.at[to_x, to_y, to_z],
                send.at[1, index],
                recv.at[1, index],
                step,
            )
        )
        slot = ((1 - dx) * 3 + (1 - dy)) * 3 + (1 - dz)
        copies.append(remote(mid_ref, mids_ref.at[slot], send.at[2, index], recv.at[2, index], step))
    for copy in local:
        copy.wait()
    for copy in first:
        copy.wait()
    second = [
        remote(tops_ref.at[ix, iy], tops_ref.at[ix, iy], gsend.at[8 + k], grecv.at[8 + k], (0, k, 0))
        for k in range(1, ny)
    ]
    for copy in second:
        copy.wait()
    third = [
        remote(tops_ref.at[ix], tops_ref.at[ix], gsend.at[16 + k], grecv.at[16 + k], (k, 0, 0)) for k in range(1, nx)
    ]
    for copy in third:
        copy.wait()
    for copy in copies:
        copy.wait()


def near_kernel(ext_ref, out_ref, table_ref):
    lane = lax.broadcasted_iota(jnp.int32, (4, LANES), 1)
    lane8 = lax.broadcasted_iota(jnp.int32, (8, LANES), 1)
    row8 = lax.broadcasted_iota(jnp.int32, (8, LANES), 0)
    picks = [(lane8 // SLOTS + turn) % 4 * SLOTS + row8 for turn in (3, 0, 1)]

    def fill(cell, carry):
        x, y = cell // 6, cell % 6
        before, here, after = ext_ref[x, y, 0], ext_ref[x, y, 1], ext_ref[x, y, 2]
        sources = (jnp.where(lane >= 96, before, here), here, jnp.where(lane < 32, after, here))
        for ez in range(3):
            for c in range(4):
                wide = jnp.broadcast_to(sources[ez][c : c + 1], (8, LANES))
                for group in range(4):
                    table_ref[cell, ez, c, group * 8 : group * 8 + 8, :] = jnp.take_along_axis(
                        wide, picks[ez] + group * 8, axis=1
                    )
        return carry

    lax.fori_loop(0, 36, fill, 0)

    def target(cell, carry):
        x, y = cell // 4, cell % 4
        mine = ext_ref[x + 1, y + 1, 1]
        wide = [jnp.broadcast_to(mine[c : c + 1], (8, LANES)) for c in range(4)]

        def around(step, sums):
            ex, ey = step // 3, step % 3
            here_x = wide[0] - (ex - 1).astype(F32)
            here_y = wide[1] - (ey - 1).astype(F32)
            other = (x + ex) * 6 + y + ey
            potential, along_x, along_y, along_z = sums
            for ez in range(3):
                here_z = wide[2] - float(ez - 1)
                for group in range(4):
                    span = pl.ds(group * 8, 8)
                    delta_x = here_x - table_ref[other, ez, 0, span, :]
                    delta_y = here_y - table_ref[other, ez, 1, span, :]
                    delta_z = here_z - table_ref[other, ez, 2, span, :]
                    distance = delta_x * delta_x + delta_y * delta_y + (delta_z * delta_z + SOFTENING)
                    inverse = lax.rsqrt(distance)
                    weight = table_ref[other, ez, 3, span, :] * inverse
                    cubic = weight * (inverse * inverse)
                    potential = potential + weight
                    along_x = along_x + cubic * delta_x
                    along_y = along_y + cubic * delta_y
                    along_z = along_z + cubic * delta_z
            return potential, along_x, along_y, along_z

        zero = jnp.zeros((8, LANES), F32)
        sums = lax.fori_loop(0, 9, around, (zero, zero, zero, zero))
        itself = mine[3:4] * lax.rsqrt(jnp.full((1, LANES), SOFTENING, F32))
        rows = [jnp.sum(part, axis=0, keepdims=True) for part in sums]
        rows[0] = rows[0] - itself
        for c in range(4):
            out_ref[x, y, c : c + 1, :] = rows[c]
        return carry

    lax.fori_loop(0, 16, target, 0)


def far_kernel(
    far_ref,
    wide_ref,
    mids_ref,
    tops_ref,
    near_ref,
    data_ref,
    live_ref,
    exps_ref,
    slope_ref,
    up_ref,
    down_ref,
    lattice_ref,
    pot_ref,
    field_ref,
    rows_ref,
    tiles_ref,
    upper_ref,
    ring_ref,
    acc_ref,
    local_ref,
    high_ref,
    low_ref,
):
    ix, iy, iz = lax.axis_index("gx"), lax.axis_index("gy"), lax.axis_index("gz")
    top_x, top_y, top_z = ix // 2, iy // 2, iz // 2
    octant_own = (ix % 2) * 4 + (iy % 2) * 2 + iz % 2

    def gather(n, carry):
        step_x, step_y, step_z = n // 9, n // 3 % 3, n % 3
        for parent in range(8):
            px, py, pz = parent >> 2, parent >> 1 & 1, parent & 1
            rows_ref[pl.ds(n * 128 + parent, 8, stride=16), :] = wide_ref[px + step_x, py + step_y, pz + step_z]
        rows_ref[pl.ds(n * 128 + 8, 8, stride=16), :] = mids_ref[n]
        far_x = lax.rem(top_x + step_x + 3, 4) * 2
        far_y = lax.rem(top_y + step_y + 1, 2) * 2
        far_z = lax.rem(top_z + step_z + 3, 4) * 2
        for octant in range(8):
            ox, oy, oz = octant >> 2, octant >> 1 & 1, octant & 1
            base = n * 128 + octant * 16
            rows_ref[pl.ds(base + 9, 1), :] = tops_ref[far_x + ox, far_y + oy, far_z + oz]
            rows_ref[pl.ds(base + 10, 6), :] = jnp.zeros((6, LANES), F32)
        return carry

    lax.fori_loop(0, 27, gather, 0)

    def convert(n, carry):
        for octant in range(8):
            start = pl.multiple_of(n * 128 + octant * 16, 16)
            tiles_ref[n * 8 + octant] = rows_ref[pl.ds(start, 16), :].astype(BF16)
        return carry

    lax.fori_loop(0, 27, convert, 0)

    for octant in range(8):
        ox, oy, oz = octant >> 2, octant >> 1 & 1, octant & 1
        for box in range(32):
            bx, by, bz = box >> 3, box >> 2 & 1, box & 3
            upper_ref[octant, box : box + 1, :] = tops_ref[2 * bx + ox, 2 * by + oy, 2 * bz + oz]
    coarse = jnp.zeros((32, TERMS), F32)
    for octant in range(8):
        coarse = coarse + split_nt(upper_ref[octant][:, :TERMS], up_ref[octant])
    root = jnp.sum(coarse, axis=0, keepdims=True)
    lattice_term = split_nt(root, lattice_ref[...])
    row = lax.broadcasted_iota(jnp.int32, (32, 32), 0)
    column = lax.broadcasted_iota(jnp.int32, (32, 32), 1)
    wanted = (
        (row // 8 + top_x) % 4 * 8 + (row // 4 % 2 + top_y) % 2 * 4 + (row % 4 + top_z) % 4
    )
    turned = jnp.dot(
        (wanted == column).astype(F32).astype(BF16), widen(coarse).astype(BF16), preferred_element_type=F32
    )
    for box in range(32):
        ring_ref[box] = jnp.broadcast_to(turned[box : box + 1], (16, LANES)).astype(BF16)

    shifts = offset_table()
    empty = jnp.zeros((16, LANES), BF16)
    total = jnp.zeros((144, TERMS), F32)
    for start in range(0, OFFSETS, CHUNK):
        columns, operators = [], []
        for index in range(start, min(start + CHUNK, OFFSETS)):
            shift = shifts[index]
            parts = []
            for parity in range(8):
                odd = (parity >> 2, parity >> 1 & 1, parity & 1)
                place = [shift[axis] + odd[axis] for axis in range(3)]
                if all(-2 <= c <= 3 for c in place):
                    around = [(c + 2) // 2 for c in place]
                    inner = [(c + 2) % 2 for c in place]
                    cell = ((around[0] * 3 + around[1]) * 3 + around[2]) * 8
                    parts.append(tiles_ref[cell + inner[0] * 4 + inner[1] * 2 + inner[2]])
                else:
                    parts.append(empty)
            parts.append(ring_ref[shift[0] % 4 * 8 + shift[1] % 2 * 4 + shift[2] % 4])
            columns.append(jnp.concatenate(parts, axis=0))
            begin = index * TERMS
            if begin + LANES <= far_ref.shape[1]:
                operators.append(far_ref[:, begin : begin + LANES])
            else:
                tail = far_ref[:, begin : begin + TERMS]
                operators.append(jnp.concatenate([tail, jnp.zeros((TERMS, LANES - TERMS), BF16)], axis=1))
        total = total + lanes_nt(jnp.concatenate(columns, axis=1), jnp.concatenate(operators, axis=1))
    acc_ref[...] = widen(total)

    local_top = 0.125 * (acc_ref[128:129, :][:, :TERMS] + lattice_term)
    local_upper = 0.25 * acc_ref[pl.ds(octant_own * 16 + 9, 1), :][:, :TERMS] + split_nt(
        local_top, down_ref[octant_own]
    )
    upper_wide = jnp.broadcast_to(local_upper, (8, TERMS))
    which = lax.broadcasted_iota(jnp.int32, (8, TERMS), 0)
    local_mid = 0.5 * acc_ref[pl.ds(8, 8, stride=16), :][:, :TERMS]
    for octant in range(8):
        local_mid = local_mid + jnp.where(which == octant, split_nt(upper_wide, down_ref[octant]), 0.0)
    for octant in range(8):
        local = acc_ref[octant * 16 : octant * 16 + 8, :][:, :TERMS] + split_nt(local_mid, down_ref[octant])
        local_ref[octant * 8 : octant * 8 + 8, :] = widen(local)
    local_leaf = local_ref[...]
    upper, lower = halves(local_leaf[:, :TERMS])
    slopes = jnp.dot(upper, slope_ref[...], preferred_element_type=F32) + jnp.dot(
        lower, slope_ref[...], preferred_element_type=F32
    )
    parts = [local_leaf] + [slopes[:, c * LANES : (c + 1) * LANES] for c in range(3)]
    split_parts = [halves(part[:, :KPAD]) for part in parts]

    def rows_of(x, y):
        return tuple(data_ref[x, y, c : c + 1, :] for c in range(3))

    monomial_tiles(rows_of, exps_ref, high_ref, low_ref)
    row = lax.broadcasted_iota(jnp.int32, (16, LANES), 0)
    lane = lax.broadcasted_iota(jnp.int32, (16, LANES), 1)
    for parity in range(4):
        span = slice(parity * 16, parity * 16 + 16)
        coef_high = jnp.concatenate([part[0][span] for part in split_parts], axis=0)
        coef_low = jnp.concatenate([part[1][span] for part in split_parts], axis=0)
        coef = jnp.concatenate([coef_high, coef_low], axis=0)
        for group in range(4):
            x, y = (group >> 1) * 2 + (parity >> 1), (group & 1) * 2 + (parity & 1)
            tile = group * 4 + parity
            lanes = slice(tile * LANES, tile * LANES + LANES)
            both = jnp.dot(coef, high_ref[:, lanes], preferred_element_type=F32)
            value = both[:64] + both[64:] + jnp.dot(coef_high, low_ref[:, lanes], preferred_element_type=F32)
            hit = (row // 8 == lane // 32 % 2) & (row % 8 == group * 2 + lane // 64)
            sums = [
                jnp.sum(jnp.where(hit, value[16 * c : 16 * c + 16], 0.0), axis=0, keepdims=True) for c in range(4)
            ]
            live = live_ref[x, y : y + 1, :]
            pot_ref[x, y : y + 1, :] = (near_ref[x, y, 0:1, :] + sums[0]) * live
            for c in range(3):
                field_ref[c, x, y : y + 1, :] = (near_ref[x, y, c + 1 : c + 2, :] - sums[c + 1]) * live


VMEM = pl.BlockSpec(memory_space=pltpu.VMEM)


def shape(*dims):
    return jax.ShapeDtypeStruct(dims, F32)


def moments_call(positions, charges, counts, exps, moment_shift):
    return pl.pallas_call(
        moments_kernel,
        out_shape=(shape(4, 4, 4, LANES), shape(4, 4, LANES), shape(64, LANES), shape(8, LANES), shape(1, LANES)),
        in_specs=[VMEM] * 5,
        out_specs=(VMEM,) * 5,
        scratch_shapes=[pltpu.VMEM((KPAD, 2048), BF16)] * 2,
        name="moments",
    )(positions, charges, counts, exps, moment_shift)


def exchange_call(sizes, data, leaf, mid, top):
    dma = pltpu.SemaphoreType.DMA
    return pl.pallas_call(
        functools.partial(exchange_kernel, *sizes),
        out_shape=(
            shape(6, 6, 3, 4, LANES),
            shape(4, 4, 4, 8, LANES),
            shape(27, 8, LANES),
            shape(*sizes, 1, LANES),
        ),
        in_specs=[VMEM] * 4,
        out_specs=(VMEM,) * 4,
        scratch_shapes=[dma((3, 26)), dma((3, 26)), dma((24,)), dma((24,)), dma((4,))],
        compiler_params=pltpu.CompilerParams(collective_id=0, has_side_effects=True),
        name="exchange",
    )(data, leaf, mid, top)


def near_call(ext):
    return pl.pallas_call(
        near_kernel,
        out_shape=shape(4, 4, 4, LANES),
        in_specs=[VMEM],
        out_specs=VMEM,
        scratch_shapes=[pltpu.VMEM((36, 3, 4, SLOTS, LANES), F32)],
        name="near",
    )(ext)


def far_call(*operands):
    return pl.pallas_call(
        far_kernel,
        out_shape=(shape(4, 4, LANES), shape(3, 4, 4, LANES)),
        in_specs=[VMEM] * 12,
        out_specs=(VMEM,) * 2,
        scratch_shapes=[
            pltpu.VMEM((27 * 128, LANES), F32),
            pltpu.VMEM((216, 16, LANES), BF16),
            pltpu.VMEM((8, 32, LANES), F32),
            pltpu.VMEM((32, 16, LANES), BF16),
            pltpu.VMEM((144, LANES), F32),
            pltpu.VMEM((64, LANES), F32),
            pltpu.VMEM((KPAD, 2048), BF16),
            pltpu.VMEM((KPAD, 2048), BF16),
        ],
        name="far",
    )(*operands)


def solution(mesh):
    sizes = tuple(mesh.shape[axis] for axis in ("gx", "gy", "gz"))

    def per_device(
        positions, charges, counts, moment_shift, far_operators, local_shift, lattice_operator
    ):
        exps = jnp.asarray(exponent_planes())
        slope = jnp.asarray(slope_matrix()).astype(BF16)
        data, live, leaf, mid, top = moments_call(positions, charges, counts, exps, moment_shift)
        ext, wide, mids, tops = exchange_call(sizes, data, leaf.reshape(2, 2, 2, 8, LANES), mid, top)
        near = near_call(ext)
        return far_call(
            far_operators,
            wide,
            mids,
            tops,
            near,
            data,
            live,
            exps,
            slope,
            moment_shift,
            local_shift,
            lattice_operator,
        )

    placed = (
        P(None, "gx", "gy", "gz"),
        P("gx", "gy", "gz"),
        P("gx", "gy", "gz"),
        P(),
        P(),
        P(),
        P(),
    )
    return jax.shard_map(
        per_device,
        mesh=mesh,
        in_specs=placed,
        out_specs=(P("gx", "gy", "gz"), P(None, "gx", "gy", "gz")),
        check_vma=False,
    )
```

profile of v0, /device:TPU:1, one launch (start us, length us, event | category | flops | bytes accessed | tf_op | source)
XLA Modules:
  0.0 61.6 jit_solution(16868149235973990966)
XLA Ops:
  0.6 1.6 %copy.11.up_ref = bf16[8,81,81]{2,1,0:T(8,128)(2,1)} copy(bf16[8,81,81]{2,0,1:T(8,128)(2,1)} %param.12) | data formatting | bytes 209952 | tf_op args[3]
  2.2 3.6 %moments.1 = (f32[4,4,4,128]{3,2,1,0:T(4,128)}, f32[4,4,128]{2,1,0:T(4,128)}, f32[64,128]{1,0:T(8,128)}, f32[8,128]{1,0:T(8,128)}, f32[1,128]{1,0:T(1,128)}) custom-call(f32[3,4,4,128]{3,2,1,0:T(4,128)} %pos_ref.1, f32[4,4,128]{2,1,0:T(4,128)} %chg_ref.1, s32[4,4,4]{2,1,0:T(4,128)} %cnt_ref.1, s32[4,96,128]{2,1,0:T(8,128)} %constant.4.clone.exps_ref, ...), custom_call_target="tpu_custom_call" | custom-call | tf_op jit(solution)/shard_map/moments/pallas_call | solution.py:477
  5.9 25.7 %exchange.1 = (f32[6,6,3,4,128]{4,3,2,1,0:T(4,128)}, f32[4,4,4,8,128]{4,3,2,1,0:T(8,128)}, f32[27,8,128]{2,1,0:T(8,128)}, f32[8,4,8,1,128]{4,3,2,1,0:T(1,128)}) custom-call(f32[4,4,4,128]{3,2,1,0:T(4,128)} %get-tuple-element.11.data_ref, f32[2,2,2,8,128]{4,3,2,1,0:T(8,128)} %bitcast.1, f32[8,128]{1,0:T(8,128)} %get-tuple-element.13.mid_ref, ...), custom_call_target="tpu_custom_call" | custom-call | tf_op jit(solution)/shard_map/exchange/pallas_call | solution.py:489
  31.6 16.7 %near.1.near_ref = f32[4,4,4,128]{3,2,1,0:T(4,128)} custom-call(f32[6,6,3,4,128]{4,3,2,1,0:T(4,128)} %get-tuple-element.18.ext_ref), custom_call_target="tpu_custom_call" | custom-call | tf_op jit(solution)/shard_map/near/pallas_call | solution.py:506
  48.2 1.6 %copy.13.down_ref = bf16[8,81,81]{2,1,0:T(8,128)(2,1)} copy(bf16[8,81,81]{2,0,1:T(8,128)(2,1)} %param.14) | data formatting | bytes 209952 | tf_op args[5]
  49.8 11.7 %far.1 = (f32[4,4,128]{2,1,0:T(4,128)}, f32[3,4,4,128]{3,2,1,0:T(4,128)}) custom-call(bf16[81,25600]{1,0:T(8,128)(2,1)} %far_ref.1, f32[4,4,4,8,128]{4,3,2,1,0:T(8,128)} %get-tuple-element.15.wide_ref, f32[27,8,128]{2,1,0:T(8,128)} %get-tuple-element.16.mids_ref, f32[8,4,8,1,128]{4,3,2,1,0:T(1,128)} %get-tuple-element.17.tops_ref, ...), custom_call_target="tpu_custom_call" | custom-call | tf_op jit(solution)/shard_map/far/pallas_call | solution.py:517
where the time goes:
time: 61.8 us; the launch traced here: 61.6 us
  Pallas kernels  57.7 us (93%)
  local copies, waits for them, and re-layouts  3.22 us (5%)
  between operations  0.64 us (1%)
    pallas_call x1, Pallas kernels, exchange_call(): pl.pallas_call(functools.partial(exchange_kernel, *sizes), out_shape=(sha...  25.7 us
    pallas_call x1, Pallas kernels, near_call(): pl.pallas_call(near_kernel, out_shape=shape(4, 4, 4, LANES), in_specs=[VM...  16.7 us
    pallas_call x1, Pallas kernels, far_call(): pl.pallas_call(far_kernel, out_shape=(shape(4, 4, LANES), shape(3, 4, 4,...  11.7 us
    pallas_call x1, Pallas kernels, moments_call(): pl.pallas_call(moments_kernel, out_shape=(shape(4, 4, 4, LANES), shape(4,...  3.62 us
    unnamed x2, local copies, waits for them, and re-layouts  3.22 us

commit v1 on v0

--- a/solution.py
+++ b/solution.py
@@ -106,9 +106,15 @@
         low_ref[:, tile * LANES : (tile + 1) * LANES] = lower
 
 
-def moments_kernel(
-    pos_ref, chg_ref, cnt_ref, exps_ref, up_ref, data_ref, live_ref, leaf_ref, mid_ref, top_ref, high_ref, low_ref
-):
+def octant_operators(native_ref, rows_ref):
+    rows_ref[:, :TERMS] = native_ref[...].astype(F32).reshape(TERMS * 8, TERMS)
+
+
+def octant_operator(rows_ref, octant):
+    return rows_ref[pl.ds(octant, TERMS, stride=8), :][:, :TERMS].astype(BF16)
+
+
+def prepare(pos_ref, chg_ref, cnt_ref, data_ref, live_ref):
     counts = jnp.concatenate([cnt_ref[x] for x in range(4)], axis=0).astype(F32).astype(BF16)
     spread = (
         lax.broadcasted_iota(jnp.int32, (4, LANES), 1) // SLOTS == lax.broadcasted_iota(jnp.int32, (4, LANES), 0)
@@ -123,10 +129,12 @@
                 data_ref[x, y, c : c + 1, :] = pos_ref[c, x, y : y + 1, :]
             data_ref[x, y, 3:4, :] = chg_ref[x, y : y + 1, :] * live[4 * x + y : 4 * x + y + 1]
 
-    def rows_of(x, y):
-        return tuple(pos_ref[c, x, y : y + 1, :] for c in range(3))
-
-    monomial_tiles(rows_of, exps_ref, high_ref, low_ref)
+
+def rows_from(data_ref):
+    return lambda x, y: tuple(data_ref[x, y, c : c + 1, :] for c in range(3))
+
+
+def moments(data_ref, operator_rows, leaf_ref, mid_ref, top_ref, high_ref, low_ref):
     row = lax.broadcasted_iota(jnp.int32, (16, LANES), 0)
     lane = lax.broadcasted_iota(jnp.int32, (16, LANES), 1)
     for group in range(4):
@@ -140,16 +148,20 @@
         upper, lower = halves(jnp.concatenate(pieces, axis=1))
         span = slice(group * 512, group * 512 + 512)
         both = lanes_nt(jnp.concatenate([upper, lower], axis=0), high_ref[:, span])
-        total = both[:16] + both[16:] + lanes_nt(upper, low_ref[:, span])
-        leaf_ref[group * 16 : group * 16 + 16, :] = widen(total)
+        total = widen(both[:16] + both[16:] + lanes_nt(upper, low_ref[:, span]))
+        leaf_ref[px, py, 0] = total[:8]
+        leaf_ref[px, py, 1] = total[8:]
     mid = jnp.zeros((8, TERMS), F32)
+    top = jnp.zeros((8, TERMS), F32)
+    which = lax.broadcasted_iota(jnp.int32, (8, TERMS), 0)
+    tiles = [leaf_ref[p >> 2, p >> 1 & 1, p & 1] for p in range(8)]
+    operators = [octant_operator(operator_rows, octant) for octant in range(8)]
     for octant in range(8):
-        mid = mid + split_nt(leaf_ref[pl.ds(octant, 8, stride=8), :][:, :TERMS], up_ref[octant])
+        rows = jnp.concatenate([tile[octant : octant + 1] for tile in tiles], axis=0)
+        mid = mid + split_nt(rows[:, :TERMS], operators[octant])
     mid_ref[...] = widen(mid)
-    which = lax.broadcasted_iota(jnp.int32, (8, TERMS), 0)
-    top = jnp.zeros((8, TERMS), F32)
     for octant in range(8):
-        top = top + jnp.where(which == octant, split_nt(mid, up_ref[octant]), 0.0)
+        top = top + jnp.where(which == octant, split_nt(mid, operators[octant]), 0.0)
     top_ref[...] = widen(jnp.sum(top, axis=0, keepdims=True))
 
 
@@ -166,8 +178,114 @@
     return pl.ds(0, 1), pl.ds(first + own, 1)
 
 
-def exchange_kernel(
-    nx, ny, nz, data_ref, leaf_ref, mid_ref, top_ref, ext_ref, wide_ref, mids_ref, tops_ref, send, recv, gsend, grecv, own
+def fill_rows(ext_ref, turned_ref):
+    lane = lax.broadcasted_iota(jnp.int32, (4, LANES), 1)
+
+    def along_x(x, carry):
+        def along_y(y, inner):
+            before, here, after = ext_ref[x, y, 0], ext_ref[x, y, 1], ext_ref[x, y, 2]
+            turned_ref[x, y, 0] = pltpu.roll(jnp.where(lane >= 96, before, here), 32, 1)
+            turned_ref[x, y, 1] = here
+            turned_ref[x, y, 2] = pltpu.roll(jnp.where(lane < 32, after, here), 96, 1)
+            return inner
+
+        return lax.fori_loop(0, 6, along_y, carry)
+
+    lax.fori_loop(0, 6, along_x, 0)
+
+
+def fill_table(turned_ref, table_ref):
+    lane = lax.broadcasted_iota(jnp.int32, (8, LANES), 1)
+    base = lane // SLOTS * SLOTS + lax.broadcasted_iota(jnp.int32, (8, LANES), 0)
+    for group in range(4):
+        pick = base + group * 8
+
+        def along_x(x, carry):
+            def along_y(y, inner):
+                for ez in range(3):
+                    rows = turned_ref[x, y, ez]
+                    for c in range(4):
+                        table_ref[x, y, ez, c, group * 8 : group * 8 + 8, :] = jnp.take_along_axis(
+                            jnp.broadcast_to(rows[c : c + 1], (8, LANES)), pick, axis=1
+                        )
+                return inner
+
+            return lax.fori_loop(0, 6, along_y, carry)
+
+        lax.fori_loop(0, 6, along_x, 0)
+
+
+def near_rows(first, last, data_ref, table_ref, out_ref):
+    def along_x(x, carry):
+        def along_y(y, inner):
+            mine = data_ref[x, y]
+            wide = [jnp.broadcast_to(mine[c : c + 1], (8, LANES)) for c in range(3)]
+            here_y = [wide[1] - float(ey - 1) for ey in range(3)]
+            here_z = [wide[2] - float(ez - 1) for ez in range(3)]
+
+            def around(ex, sums):
+                here_x = wide[0] - (ex - 1).astype(F32)
+                potential, field_x, field_y, field_z = sums
+                for ey in range(3):
+                    for ez in range(3):
+                        for group in range(4):
+                            span = pl.ds(group * 8, 8)
+                            delta_x = here_x - table_ref[x + ex, y + ey, ez, 0, span, :]
+                            delta_y = here_y[ey] - table_ref[x + ex, y + ey, ez, 1, span, :]
+                            delta_z = here_z[ez] - table_ref[x + ex, y + ey, ez, 2, span, :]
+                            distance = delta_x * delta_x + delta_y * delta_y + (delta_z * delta_z + SOFTENING)
+                            inverse = lax.rsqrt(distance)
+                            weight = table_ref[x + ex, y + ey, ez, 3, span, :] * inverse
+                            cubic = weight * (inverse * inverse)
+                            potential = potential + weight
+                            field_x = field_x + cubic * delta_x
+                            field_y = field_y + cubic * delta_y
+                            field_z = field_z + cubic * delta_z
+                return potential, field_x, field_y, field_z
+
+            zero = jnp.zeros((8, LANES), F32)
+            sums = lax.fori_loop(0, 3, around, (zero, zero, zero, zero))
+            itself = mine[3:4] * lax.rsqrt(jnp.full((1, LANES), SOFTENING, F32))
+            rows = [jnp.sum(part, axis=0, keepdims=True) for part in sums]
+            rows[0] = rows[0] - itself
+            for c in range(4):
+                out_ref[x, y, c : c + 1, :] = rows[c]
+            return inner
+
+        return lax.fori_loop(0, 4, along_y, carry)
+
+    lax.fori_loop(first, last, along_x, 0)
+
+
+def pairs_kernel(
+    nx,
+    ny,
+    nz,
+    pos_ref,
+    chg_ref,
+    cnt_ref,
+    exps_ref,
+    up_ref,
+    near_ref,
+    data_ref,
+    live_ref,
+    wide_ref,
+    mids_ref,
+    tops_ref,
+    ext_ref,
+    leaf_ref,
+    mid_ref,
+    top_ref,
+    operator_rows,
+    high_ref,
+    low_ref,
+    turned_ref,
+    table_ref,
+    send,
+    recv,
+    gsend,
+    grecv,
+    own,
 ):
     ix, iy, iz = lax.axis_index("gx"), lax.axis_index("gy"), lax.axis_index("gz")
 
@@ -178,13 +296,19 @@
             "gz": lax.rem(iz + (dz + nz), nz),
         }
 
-    partners = list(DIRECTIONS)
-    partners += [(0, 0, k) for k in range(2, nz - 1)]
-    partners += [(0, k, 0) for k in range(2, ny - 1)]
-    partners += [(k, 0, 0) for k in range(2, nx - 1)]
+    plane = [(0, b, c) for b in range(ny) for c in range(nz) if b or c]
+    line = [(a, 0, 0) for a in range(1, nx)]
+    wrapped = lambda step: (step[0] % nx, step[1] % ny, step[2] % nz)
+    partners = sorted({wrapped(step) for step in DIRECTIONS} | set(plane) | set(line))
     barrier = pltpu.get_barrier_semaphore()
     for step in partners:
         pl.semaphore_signal(barrier, inc=1, device_id=at(*step), device_id_type=MESH)
+
+    prepare(pos_ref, chg_ref, cnt_ref, data_ref, live_ref)
+    octant_operators(up_ref, operator_rows)
+    monomial_tiles(rows_from(data_ref), exps_ref, high_ref, low_ref)
+    moments(data_ref, operator_rows, leaf_ref, mid_ref, top_ref, high_ref, low_ref)
+
     pl.semaphore_wait(barrier, len(partners))
 
     def remote(src, dst, ssem, rsem, step):
@@ -194,125 +318,49 @@
         copy.start()
         return copy
 
-    first = [
-        remote(top_ref, tops_ref.at[ix, iy, iz], gsend.at[k], grecv.at[k], (0, 0, k)) for k in range(1, nz)
-    ]
     local = [
-        pltpu.make_async_copy(top_ref, tops_ref.at[ix, iy, iz], own.at[0]),
-        pltpu.make_async_copy(mid_ref, mids_ref.at[13], own.at[1]),
-        pltpu.make_async_copy(leaf_ref, wide_ref.at[pl.ds(1, 2), pl.ds(1, 2), pl.ds(1, 2)], own.at[2]),
-        pltpu.make_async_copy(data_ref, ext_ref.at[pl.ds(1, 4), pl.ds(1, 4), 1], own.at[3]),
+        pltpu.make_async_copy(data_ref, ext_ref.at[pl.ds(1, 4), pl.ds(1, 4), 1], own.at[0]),
+        pltpu.make_async_copy(leaf_ref, wide_ref.at[pl.ds(1, 2), pl.ds(1, 2), pl.ds(1, 2)], own.at[1]),
+        pltpu.make_async_copy(mid_ref, mids_ref.at[13], own.at[2]),
+        pltpu.make_async_copy(top_ref, tops_ref.at[ix, iy, iz], own.at[3]),
     ]
     for copy in local:
         copy.start()
-    copies = []
+    halo = []
     for index, step in enumerate(DIRECTIONS):
         dx, dy, dz = step
         from_x, to_x = span_of(dx, 4, 1)
         from_y, to_y = span_of(dy, 4, 1)
-        copies.append(
-            remote(
-                data_ref.at[from_x, from_y],
-                ext_ref.at[to_x, to_y, 1 - dz],
-                send.at[0, index],
-                recv.at[0, index],
-                step,
-            )
-        )
+        src, dst = data_ref.at[from_x, from_y], ext_ref.at[to_x, to_y, 1 - dz]
+        halo.append(remote(src, dst, send.at[0, index], recv.at[0, index], step))
+    first = [
+        remote(top_ref, tops_ref.at[ix, iy, iz], gsend.at[k], grecv.at[k], step) for k, step in enumerate(plane)
+    ]
+    boxes = []
     for index, step in enumerate(DIRECTIONS):
-        dx, dy, dz = step
-        from_x, to_x = span_of(dx, 2, 1)
-        from_y, to_y = span_of(dy, 2, 1)
-        from_z, to_z = span_of(dz, 2, 1)
-        copies.append(
-            remote(
-                leaf_ref.at[from_x, from_y, from_z],
-                wide_ref.at[to_x, to_y, to_z],
-                send.at[1, index],
-                recv.at[1, index],
-                step,
-            )
-        )
-        slot = ((1 - dx) * 3 + (1 - dy)) * 3 + (1 - dz)
-        copies.append(remote(mid_ref, mids_ref.at[slot], send.at[2, index], recv.at[2, index], step))
+        spans = [span_of(d, 2, 1) for d in step]
+        src = leaf_ref.at[spans[0][0], spans[1][0], spans[2][0]]
+        dst = wide_ref.at[spans[0][1], spans[1][1], spans[2][1]]
+        boxes.append(remote(src, dst, send.at[1, index], recv.at[1, index], step))
+        slot = ((1 - step[0]) * 3 + (1 - step[1])) * 3 + (1 - step[2])
+        boxes.append(remote(mid_ref, mids_ref.at[slot], send.at[2, index], recv.at[2, index], step))
     for copy in local:
         copy.wait()
+    for copy in halo:
+        copy.wait()
+    fill_rows(ext_ref, turned_ref)
+    fill_table(turned_ref, table_ref)
     for copy in first:
         copy.wait()
     second = [
-        remote(tops_ref.at[ix, iy], tops_ref.at[ix, iy], gsend.at[8 + k], grecv.at[8 + k], (0, k, 0))
-        for k in range(1, ny)
+        remote(tops_ref.at[ix], tops_ref.at[ix], gsend.at[32 + k], grecv.at[32 + k], step)
+        for k, step in enumerate(line)
     ]
+    near_rows(0, 4, data_ref, table_ref, near_ref)
     for copy in second:
         copy.wait()
-    third = [
-        remote(tops_ref.at[ix], tops_ref.at[ix], gsend.at[16 + k], grecv.at[16 + k], (k, 0, 0)) for k in range(1, nx)
-    ]
-    for copy in third:
+    for copy in boxes:
         copy.wait()
-    for copy in copies:
-        copy.wait()
-
-
-def near_kernel(ext_ref, out_ref, table_ref):
-    lane = lax.broadcasted_iota(jnp.int32, (4, LANES), 1)
-    lane8 = lax.broadcasted_iota(jnp.int32, (8, LANES), 1)
-    row8 = lax.broadcasted_iota(jnp.int32, (8, LANES), 0)
-    picks = [(lane8 // SLOTS + turn) % 4 * SLOTS + row8 for turn in (3, 0, 1)]
-
-    def fill(cell, carry):
-        x, y = cell // 6, cell % 6
-        before, here, after = ext_ref[x, y, 0], ext_ref[x, y, 1], ext_ref[x, y, 2]
-        sources = (jnp.where(lane >= 96, before, here), here, jnp.where(lane < 32, after, here))
-        for ez in range(3):
-            for c in range(4):
-                wide = jnp.broadcast_to(sources[ez][c : c + 1], (8, LANES))
-                for group in range(4):
-                    table_ref[cell, ez, c, group * 8 : group * 8 + 8, :] = jnp.take_along_axis(
-                        wide, picks[ez] + group * 8, axis=1
-                    )
-        return carry
-
-    lax.fori_loop(0, 36, fill, 0)
-
-    def target(cell, carry):
-        x, y = cell // 4, cell % 4
-        mine = ext_ref[x + 1, y + 1, 1]
-        wide = [jnp.broadcast_to(mine[c : c + 1], (8, LANES)) for c in range(4)]
-
-        def around(step, sums):
-            ex, ey = step // 3, step % 3
-            here_x = wide[0] - (ex - 1).astype(F32)
-            here_y = wide[1] - (ey - 1).astype(F32)
-            other = (x + ex) * 6 + y + ey
-            potential, along_x, along_y, along_z = sums
-            for ez in range(3):
-                here_z = wide[2] - float(ez - 1)
-                for group in range(4):
-                    span = pl.ds(group * 8, 8)
-                    delta_x = here_x - table_ref[other, ez, 0, span, :]
-                    delta_y = here_y - table_ref[other, ez, 1, span, :]
-                    delta_z = here_z - table_ref[other, ez, 2, span, :]
-                    distance = delta_x * delta_x + delta_y * delta_y + (delta_z * delta_z + SOFTENING)
-                    inverse = lax.rsqrt(distance)
-                    weight = table_ref[other, ez, 3, span, :] * inverse
-                    cubic = weight * (inverse * inverse)
-                    potential = potential + weight
-                    along_x = along_x + cubic * delta_x
-                    along_y = along_y + cubic * delta_y
-                    along_z = along_z + cubic * delta_z
-            return potential, along_x, along_y, along_z
-
-        zero = jnp.zeros((8, LANES), F32)
-        sums = lax.fori_loop(0, 9, around, (zero, zero, zero, zero))
-        itself = mine[3:4] * lax.rsqrt(jnp.full((1, LANES), SOFTENING, F32))
-        rows = [jnp.sum(part, axis=0, keepdims=True) for part in sums]
-        rows[0] = rows[0] - itself
-        for c in range(4):
-            out_ref[x, y, c : c + 1, :] = rows[c]
-        return carry
-
-    lax.fori_loop(0, 16, target, 0)
 
 
 def far_kernel(
@@ -338,7 +386,15 @@
     local_ref,
     high_ref,
     low_ref,
+    up_rows,
+    down_rows,
+    whole_ref,
+    arrive,
 ):
+    fetch = pltpu.make_async_copy(far_ref, whole_ref, arrive.at[0])
+    fetch.start()
+    octant_operators(up_ref, up_rows)
+    octant_operators(down_ref, down_rows)
     ix, iy, iz = lax.axis_index("gx"), lax.axis_index("gy"), lax.axis_index("gz")
     top_x, top_y, top_z = ix // 2, iy // 2, iz // 2
     octant_own = (ix % 2) * 4 + (iy % 2) * 2 + iz % 2
@@ -376,7 +432,7 @@
             upper_ref[octant, box : box + 1, :] = tops_ref[2 * bx + ox, 2 * by + oy, 2 * bz + oz]
     coarse = jnp.zeros((32, TERMS), F32)
     for octant in range(8):
-        coarse = coarse + split_nt(upper_ref[octant][:, :TERMS], up_ref[octant])
+        coarse = coarse + split_nt(upper_ref[octant][:, :TERMS], octant_operator(up_rows, octant))
     root = jnp.sum(coarse, axis=0, keepdims=True)
     lattice_term = split_nt(root, lattice_ref[...])
     row = lax.broadcasted_iota(jnp.int32, (32, 32), 0)
@@ -390,6 +446,7 @@
     for box in range(32):
         ring_ref[box] = jnp.broadcast_to(turned[box : box + 1], (16, LANES)).astype(BF16)
 
+    fetch.wait()
     shifts = offset_table()
     empty = jnp.zeros((16, LANES), BF16)
     total = jnp.zeros((144, TERMS), F32)
@@ -411,25 +468,30 @@
             parts.append(ring_ref[shift[0] % 4 * 8 + shift[1] % 2 * 4 + shift[2] % 4])
             columns.append(jnp.concatenate(parts, axis=0))
             begin = index * TERMS
-            if begin + LANES <= far_ref.shape[1]:
-                operators.append(far_ref[:, begin : begin + LANES])
+            if begin + LANES <= whole_ref.shape[1]:
+                operators.append(whole_ref[:, begin : begin + LANES])
             else:
-                tail = far_ref[:, begin : begin + TERMS]
+                tail = whole_ref[:, begin : begin + TERMS]
                 operators.append(jnp.concatenate([tail, jnp.zeros((TERMS, LANES - TERMS), BF16)], axis=1))
         total = total + lanes_nt(jnp.concatenate(columns, axis=1), jnp.concatenate(operators, axis=1))
     acc_ref[...] = widen(total)
 
     local_top = 0.125 * (acc_ref[128:129, :][:, :TERMS] + lattice_term)
+    own_down = jnp.where(
+        lax.broadcasted_iota(jnp.int32, (TERMS * 8, LANES), 0) % 8 == octant_own, down_rows[...], 0.0
+    )
+    own_down = jnp.sum(own_down.reshape(TERMS, 8, LANES), axis=1)[:, :TERMS].astype(BF16)
+    downs = [octant_operator(down_rows, octant) for octant in range(8)]
     local_upper = 0.25 * acc_ref[pl.ds(octant_own * 16 + 9, 1), :][:, :TERMS] + split_nt(
-        local_top, down_ref[octant_own]
+        local_top, own_down
     )
     upper_wide = jnp.broadcast_to(local_upper, (8, TERMS))
     which = lax.broadcasted_iota(jnp.int32, (8, TERMS), 0)
     local_mid = 0.5 * acc_ref[pl.ds(8, 8, stride=16), :][:, :TERMS]
     for octant in range(8):
-        local_mid = local_mid + jnp.where(which == octant, split_nt(upper_wide, down_ref[octant]), 0.0)
+        local_mid = local_mid + jnp.where(which == octant, split_nt(upper_wide, downs[octant]), 0.0)
     for octant in range(8):
-        local = acc_ref[octant * 16 : octant * 16 + 8, :][:, :TERMS] + split_nt(local_mid, down_ref[octant])
+        local = acc_ref[octant * 16 : octant * 16 + 8, :][:, :TERMS] + split_nt(local_mid, downs[octant])
         local_ref[octant * 8 : octant * 8 + 8, :] = widen(local)
     local_leaf = local_ref[...]
     upper, lower = halves(local_leaf[:, :TERMS])
@@ -439,10 +501,7 @@
     parts = [local_leaf] + [slopes[:, c * LANES : (c + 1) * LANES] for c in range(3)]
     split_parts = [halves(part[:, :KPAD]) for part in parts]
 
-    def rows_of(x, y):
-        return tuple(data_ref[x, y, c : c + 1, :] for c in range(3))
-
-    monomial_tiles(rows_of, exps_ref, high_ref, low_ref)
+    monomial_tiles(rows_from(data_ref), exps_ref, high_ref, low_ref)
     row = lax.broadcasted_iota(jnp.int32, (16, LANES), 0)
     lane = lax.broadcasted_iota(jnp.int32, (16, LANES), 1)
     for parity in range(4):
@@ -473,51 +532,46 @@
     return jax.ShapeDtypeStruct(dims, F32)
 
 
-def moments_call(positions, charges, counts, exps, moment_shift):
-    return pl.pallas_call(
-        moments_kernel,
-        out_shape=(shape(4, 4, 4, LANES), shape(4, 4, LANES), shape(64, LANES), shape(8, LANES), shape(1, LANES)),
-        in_specs=[VMEM] * 5,
-        out_specs=(VMEM,) * 5,
-        scratch_shapes=[pltpu.VMEM((KPAD, 2048), BF16)] * 2,
-        name="moments",
-    )(positions, charges, counts, exps, moment_shift)
-
-
-def exchange_call(sizes, data, leaf, mid, top):
+def pairs_call(sizes, positions, charges, counts, exps, moment_shift):
     dma = pltpu.SemaphoreType.DMA
     return pl.pallas_call(
-        functools.partial(exchange_kernel, *sizes),
+        functools.partial(pairs_kernel, *sizes),
         out_shape=(
-            shape(6, 6, 3, 4, LANES),
+            shape(4, 4, 4, LANES),
+            shape(4, 4, 4, LANES),
+            shape(4, 4, LANES),
             shape(4, 4, 4, 8, LANES),
             shape(27, 8, LANES),
             shape(*sizes, 1, LANES),
         ),
-        in_specs=[VMEM] * 4,
-        out_specs=(VMEM,) * 4,
-        scratch_shapes=[dma((3, 26)), dma((3, 26)), dma((24,)), dma((24,)), dma((4,))],
+        in_specs=[VMEM] * 5,
+        out_specs=(VMEM,) * 6,
+        scratch_shapes=[
+            pltpu.VMEM((6, 6, 3, 4, LANES), F32),
+            pltpu.VMEM((2, 2, 2, 8, LANES), F32),
+            pltpu.VMEM((8, LANES), F32),
+            pltpu.VMEM((1, LANES), F32),
+            pltpu.VMEM((TERMS * 8, LANES), F32),
+            pltpu.VMEM((KPAD, 2048), BF16),
+            pltpu.VMEM((KPAD, 2048), BF16),
+            pltpu.VMEM((6, 6, 3, 4, LANES), F32),
+            pltpu.VMEM((6, 6, 3, 4, SLOTS, LANES), F32),
+            dma((3, 26)),
+            dma((3, 26)),
+            dma((40,)),
+            dma((40,)),
+            dma((4,)),
+        ],
         compiler_params=pltpu.CompilerParams(collective_id=0, has_side_effects=True),
-        name="exchange",
-    )(data, leaf, mid, top)
-
-
-def near_call(ext):
-    return pl.pallas_call(
-        near_kernel,
-        out_shape=shape(4, 4, 4, LANES),
-        in_specs=[VMEM],
-        out_specs=VMEM,
-        scratch_shapes=[pltpu.VMEM((36, 3, 4, SLOTS, LANES), F32)],
-        name="near",
-    )(ext)
+        name="pairs",
+    )(positions, charges, counts, exps, moment_shift)
 
 
 def far_call(*operands):
     return pl.pallas_call(
         far_kernel,
         out_shape=(shape(4, 4, LANES), shape(3, 4, 4, LANES)),
-        in_specs=[VMEM] * 12,
+        in_specs=[pl.BlockSpec(memory_space=pl.ANY)] + [VMEM] * 11,
         out_specs=(VMEM,) * 2,
         scratch_shapes=[
             pltpu.VMEM((27 * 128, LANES), F32),
@@ -528,6 +582,10 @@
             pltpu.VMEM((64, LANES), F32),
             pltpu.VMEM((KPAD, 2048), BF16),
             pltpu.VMEM((KPAD, 2048), BF16),
+            pltpu.VMEM((TERMS * 8, LANES), F32),
+            pltpu.VMEM((TERMS * 8, LANES), F32),
+            pltpu.VMEM((TERMS, 25600), BF16),
+            pltpu.SemaphoreType.DMA((1,)),
         ],
         name="far",
     )(*operands)
@@ -541,9 +599,9 @@
     ):
         exps = jnp.asarray(exponent_planes())
         slope = jnp.asarray(slope_matrix()).astype(BF16)
-        data, live, leaf, mid, top = moments_call(positions, charges, counts, exps, moment_shift)
-        ext, wide, mids, tops = exchange_call(sizes, data, leaf.reshape(2, 2, 2, 8, LANES), mid, top)
-        near = near_call(ext)
+        native_up = jnp.transpose(moment_shift, (1, 0, 2))
+        native_down = jnp.transpose(local_shift, (1, 0, 2))
+        near, data, live, wide, mids, tops = pairs_call(sizes, positions, charges, counts, exps, native_up)
         return far_call(
             far_operators,
             wide,
@@ -554,8 +612,8 @@
             live,
             exps,
             slope,
-            moment_shift,
-            local_shift,
+            native_up,
+            native_down,
             lattice_operator,
         )
 

time: 61.8 us -> 51.9 us (0.84)
  Pallas kernels: 57.7 us -> 51.1 us
  local copies, waits for them, and re-layouts: 3.22 us -> 0 us
    pallas_call x3 -> x1, Pallas kernels: 46 us -> 39.9 us  [pairs_call(): pl.pallas_call(functools.partial(pairs_kernel, *sizes), out_shape=(shape(...]
    unnamed x2 -> x0, local copies, waits for them, and re-layouts: 3.22 us -> none
where the time goes in v1:
time: 51.9 us; the launch traced here: 51.8 us
  Pallas kernels  51.1 us (98%)
  between operations  0.64 us (1%)
    pallas_call x1, Pallas kernels, pairs_call(): pl.pallas_call(functools.partial(pairs_kernel, *sizes), out_shape=(shape(...  39.9 us
    pallas_call x1, Pallas kernels, far_call(): pl.pallas_call(far_kernel, out_shape=(shape(4, 4, LANES), shape(3, 4, 4,...  11.2 us

profile of v1, /device:TPU:1, one launch (start us, length us, event | category | flops | bytes accessed | tf_op | source)
XLA Modules:
  0.0 51.8 jit_solution(5392695890158328702)
XLA Ops:
  0.6 39.9 %pairs.1 = (f32[4,4,4,128]{3,2,1,0:T(4,128)}, f32[4,4,4,128]{3,2,1,0:T(4,128)}, f32[4,4,128]{2,1,0:T(4,128)}, f32[4,4,4,8,128]{4,3,2,1,0:T(8,128)}, f32[27,8,128]{2,1,0:T(8,128)}, /*index=5*/f32[8,4,8,1,128]{4,3,2,1,0:T(1,128)}) custom-call(f32[3,4,4,128]{3,2,1,0:T(4,128)} %pos_ref.1, f32[4,4,128]{2,1,0:T(4,128)} %chg_ref.1, s32[4,4,4]{2,1,0:T(4,128)} %cnt_ref.1, ...), custom_call_target="tpu_custom_call" | custom-call | tf_op jit(solution)/shard_map/pairs/pallas_call | solution.py:537
  40.6 11.2 %far.1 = (f32[4,4,128]{2,1,0:T(4,128)}, f32[3,4,4,128]{3,2,1,0:T(4,128)}) custom-call(bf16[81,25600]{1,0:T(8,128)(2,1)} %far_ref.1, f32[4,4,4,8,128]{4,3,2,1,0:T(8,128)} %get-tuple-element.8.wide_ref, f32[27,8,128]{2,1,0:T(8,128)} %get-tuple-element.9.mids_ref, f32[8,4,8,1,128]{4,3,2,1,0:T(1,128)} %get-tuple-element.10.tops_ref, ...), custom_call_target="tpu_custom_call" | custom-call | tf_op jit(solution)/shard_map/far/pallas_call | solution.py:571

commit v2 on v1

v2 whole, which is shorter than its diff:
```python
import functools

import jax
import jax.numpy as jnp
import numpy as np
from jax import lax
from jax.experimental import pallas as pl
from jax.experimental.pallas import tpu as pltpu
from jax.sharding import PartitionSpec as P

ORDER = 8
SLOTS = 32
SOFTENING = 0.0625
TERMS = 81
KPAD = 96
LANES = 128
OFFSETS = 316
CHUNK = 4
MESH = pl.DeviceIdType.MESH
F32 = jnp.float32
BF16 = jnp.bfloat16


def offset_table():
    listed = []
    for shift_x in range(-3, 4):
        for shift_y in range(-3, 4):
            for shift_z in range(-3, 4):
                if max(abs(shift_x), abs(shift_y), abs(shift_z)) >= 2:
                    listed.append((shift_x, shift_y, shift_z))
    return listed


def admitted(shift):
    listed = []
    for parity in range(8):
        place = [shift[axis] + (parity >> (2 - axis) & 1) for axis in range(3)]
        if all(-2 <= c <= 3 for c in place):
            listed.append((parity, tuple(place)))
    return listed


def tile_of(place):
    around = [(c + 2) // 2 for c in place]
    inner = [(c + 2) % 2 for c in place]
    return ((around[0] * 3 + around[1]) * 3 + around[2]) * 8 + inner[0] * 4 + inner[1] * 2 + inner[2]


def offset_groups():
    groups = {}
    for index, shift in enumerate(offset_table()):
        groups.setdefault(tuple(p for p, _ in admitted(shift)), []).append(index)
    return sorted(groups.items(), key=lambda item: -len(item[0]))


TOP_ROWS = {0: 10, 7: 11, 3: 12, 4: 13, 1: 14, 6: 15}
EXTRA_TILES = {2: 216, 5: 217}


def top_parity(shift):
    if min(shift) > -3:
        return 0
    if max(shift) < 3:
        return 7
    fits = [parity for parity, _ in admitted(shift) if parity in TOP_ROWS]
    return fits[0] if fits else None


def exponent_list():
    listed = []
    for accumulated in range(ORDER + 1):
        for height in (0, 1):
            for power_x in range(accumulated - height + 1):
                listed.append((power_x, accumulated - height - power_x, height))
    return listed


def exponent_planes():
    planes = np.zeros((4, KPAD, LANES), np.int32)
    for row, (a, b, c) in enumerate(exponent_list()):
        planes[0, row], planes[1, row], planes[2, row], planes[3, row] = a, b, c, 1
    return planes


def slope_matrix():
    listed = exponent_list()
    place = {e: i for i, e in enumerate(listed)}
    matrix = np.zeros((TERMS, 3 * LANES), np.float32)
    for row, (a, b, c) in enumerate(listed):
        if a > 0:
            matrix[row, place[(a - 1, b, c)]] = a
        if b > 0:
            matrix[row, LANES + place[(a, b - 1, c)]] = b
        if c > 0:
            matrix[row, 2 * LANES + place[(a, b, c - 1)]] = c
    return matrix


def lanes_nt(lhs, rhs):
    return lax.dot_general(lhs, rhs, (((1,), (1,)), ((), ())), preferred_element_type=F32)


def halves(value):
    upper = value.astype(BF16)
    return upper, (value - upper.astype(F32)).astype(BF16)


def split_nt(value, rhs):
    rows = value.shape[0]
    if rows % 8:
        value = jnp.concatenate([value, jnp.zeros((8 - rows, value.shape[1]), F32)], axis=0)
    upper, lower = halves(value)
    both = lanes_nt(upper, rhs) + lanes_nt(lower, rhs)
    return both[:rows]


def widen(value):
    return jnp.concatenate([value, jnp.zeros((value.shape[0], LANES - value.shape[1]), F32)], axis=1)


def power_of(base, exponents):
    square = base * base
    fourth = square * square
    eighth = fourth * fourth
    result = jnp.where((exponents & 1) != 0, base, 1.0)
    result = result * jnp.where((exponents & 2) != 0, square, 1.0)
    result = result * jnp.where((exponents & 4) != 0, fourth, 1.0)
    return jnp.where(exponents == 8, eighth, result)


def monomial_tiles(rows_of, exps_ref, high_ref, low_ref):
    for tile in range(16):
        px, py, ox, oy = tile >> 3, tile >> 2 & 1, tile >> 1 & 1, tile & 1
        row_x, row_y, row_z = rows_of(2 * px + ox, 2 * py + oy)
        full = lambda row: jnp.broadcast_to(row - 0.5, (KPAD, LANES))
        value = power_of(full(row_x), exps_ref[0]) * power_of(full(row_y), exps_ref[1])
        value = value * jnp.where(exps_ref[2] != 0, full(row_z), 1.0)
        value = jnp.where(exps_ref[3] != 0, value, 0.0)
        upper, lower = halves(value)
        high_ref[:, tile * LANES : (tile + 1) * LANES] = upper
        low_ref[:, tile * LANES : (tile + 1) * LANES] = lower


def octant_operators(native_ref, rows_ref):
    rows_ref[:, :TERMS] = native_ref[...].astype(F32).reshape(TERMS * 8, TERMS)


def octant_operator(rows_ref, octant):
    return rows_ref[pl.ds(octant, TERMS, stride=8), :][:, :TERMS].astype(BF16)


def prepare(pos_ref, chg_ref, cnt_ref, data_ref, live_ref):
    counts = jnp.concatenate([cnt_ref[x] for x in range(4)], axis=0).astype(F32).astype(BF16)
    spread = (
        lax.broadcasted_iota(jnp.int32, (4, LANES), 1) // SLOTS == lax.broadcasted_iota(jnp.int32, (4, LANES), 0)
    ).astype(F32).astype(BF16)
    limit = jnp.dot(counts, spread, preferred_element_type=F32)
    slot_of = (lax.broadcasted_iota(jnp.int32, (16, LANES), 1) % SLOTS).astype(F32)
    live = (slot_of < limit).astype(F32)
    for x in range(4):
        live_ref[x] = live[4 * x : 4 * x + 4]
        for y in range(4):
            for c in range(3):
                data_ref[x, y, c : c + 1, :] = pos_ref[c, x, y : y + 1, :]
            data_ref[x, y, 3:4, :] = chg_ref[x, y : y + 1, :] * live[4 * x + y : 4 * x + y + 1]


def rows_from(data_ref):
    return lambda x, y: tuple(data_ref[x, y, c : c + 1, :] for c in range(3))


def moments(data_ref, operator_rows, leaf_ref, mid_ref, top_ref, high_ref, low_ref):
    row = lax.broadcasted_iota(jnp.int32, (16, LANES), 0)
    lane = lax.broadcasted_iota(jnp.int32, (16, LANES), 1)
    for group in range(4):
        px, py = group >> 1, group & 1
        pieces = []
        for tile in range(4):
            ox, oy = tile >> 1, tile & 1
            hit = (row // 8 == lane // 64) & (row % 8 == ox * 4 + oy * 2 + lane // 32 % 2)
            weight = jnp.broadcast_to(data_ref[2 * px + ox, 2 * py + oy, 3:4, :], (16, LANES))
            pieces.append(jnp.where(hit, weight, 0.0))
        upper, lower = halves(jnp.concatenate(pieces, axis=1))
        span = slice(group * 512, group * 512 + 512)
        both = lanes_nt(jnp.concatenate([upper, lower], axis=0), high_ref[:, span])
        total = widen(both[:16] + both[16:] + lanes_nt(upper, low_ref[:, span]))
        leaf_ref[px, py, 0] = total[:8]
        leaf_ref[px, py, 1] = total[8:]
    mid = jnp.zeros((8, TERMS), F32)
    top = jnp.zeros((8, TERMS), F32)
    which = lax.broadcasted_iota(jnp.int32, (8, TERMS), 0)
    tiles = [leaf_ref[p >> 2, p >> 1 & 1, p & 1] for p in range(8)]
    operators = [octant_operator(operator_rows, octant) for octant in range(8)]
    for octant in range(8):
        rows = jnp.concatenate([tile[octant : octant + 1] for tile in tiles], axis=0)
        mid = mid + split_nt(rows[:, :TERMS], operators[octant])
    mid_ref[...] = widen(mid)
    for octant in range(8):
        top = top + jnp.where(which == octant, split_nt(mid, operators[octant]), 0.0)
    top_ref[...] = widen(jnp.sum(top, axis=0, keepdims=True))


DIRECTIONS = [
    (dx, dy, dz) for dx in (-1, 0, 1) for dy in (-1, 0, 1) for dz in (-1, 0, 1) if (dx, dy, dz) != (0, 0, 0)
]


def span_of(step, own, first):
    if step == 0:
        return pl.ds(0, own), pl.ds(first, own)
    if step > 0:
        return pl.ds(own - 1, 1), pl.ds(first - 1, 1)
    return pl.ds(0, 1), pl.ds(first + own, 1)


def fill_cells(cells, ext_ref, turned_ref, table_ref):
    lane4 = lax.broadcasted_iota(jnp.int32, (4, LANES), 1)
    for x, y in cells:
        before, here, after = ext_ref[x, y, 0], ext_ref[x, y, 1], ext_ref[x, y, 2]
        turned_ref[x, y, 0] = pltpu.roll(jnp.where(lane4 >= 96, before, here), 32, 1)
        turned_ref[x, y, 1] = here
        turned_ref[x, y, 2] = pltpu.roll(jnp.where(lane4 < 32, after, here), 96, 1)
    lane = lax.broadcasted_iota(jnp.int32, (8, LANES), 1)
    base = lane // SLOTS * SLOTS + lax.broadcasted_iota(jnp.int32, (8, LANES), 0)

    def one_group(group, carry):
        pick = base + group * 8
        start = pl.multiple_of(group * 8, 8)
        for x, y in cells:
            for ez in range(3):
                for c in range(4):
                    row = jnp.broadcast_to(turned_ref[x, y, ez, c : c + 1, :], (8, LANES))
                    table_ref[x, y, ez, c, pl.ds(start, 8), :] = jnp.take_along_axis(row, pick, axis=1)
        return carry

    lax.fori_loop(0, 4, one_group, 0)


def load_wide(data_ref, x, y):
    mine = data_ref[x, y]
    return [jnp.broadcast_to(mine[c : c + 1], (8, LANES)) for c in range(3)]


def pair_sums(sums, here_x, here_y, here_z, x, y, table_ref):
    potential, field_x, field_y, field_z = sums
    for ez in range(3):
        for group in range(4):
            span = pl.ds(group * 8, 8)
            delta_x = here_x - table_ref[x, y, ez, 0, span, :]
            delta_y = here_y - table_ref[x, y, ez, 1, span, :]
            delta_z = here_z[ez] - table_ref[x, y, ez, 2, span, :]
            distance = delta_x * delta_x + delta_y * delta_y + (delta_z * delta_z + SOFTENING)
            inverse = lax.rsqrt(distance)
            weight = table_ref[x, y, ez, 3, span, :] * inverse
            cubic = weight * (inverse * inverse)
            potential = potential + weight
            field_x = field_x + cubic * delta_x
            field_y = field_y + cubic * delta_y
            field_z = field_z + cubic * delta_z
    return potential, field_x, field_y, field_z


def near_inside(rows, data_ref, table_ref, sums_ref):
    for y in rows:
        steps = [ey for ey in (-1, 0, 1) if 0 <= y + ey < 4]

        def along_x(x, carry):
            wide = load_wide(data_ref, x, y)
            here_z = [wide[2] - float(ez - 1) for ez in range(3)]

            def around(ex, sums):
                here_x = wide[0] - (ex - 1).astype(F32)
                for ey in steps:
                    sums = pair_sums(sums, here_x, wide[1] - float(ey), here_z, x + ex, y + ey + 1, table_ref)
                return sums

            zero = jnp.zeros((8, LANES), F32)
            low = 1 - jnp.minimum(x, 1)
            high = 2 + jnp.minimum(3 - x, 1)
            sums = lax.fori_loop(low, high, around, (zero, zero, zero, zero))
            for c in range(4):
                sums_ref[x, y, c] = sums[c]
            return carry

        lax.fori_loop(0, 4, along_x, 0)


def near_outside(data_ref, table_ref, sums_ref):
    for x, ex in ((0, -1), (3, 1)):

        def along_y(y, carry):
            wide = load_wide(data_ref, x, y)
            here_z = [wide[2] - float(ez - 1) for ez in range(3)]
            sums = tuple(sums_ref[x, y, c] for c in range(4))
            for ey in (-1, 0, 1):
                sums = pair_sums(
                    sums, wide[0] - float(ex), wide[1] - float(ey), here_z, x + ex + 1, y + ey + 1, table_ref
                )
            for c in range(4):
                sums_ref[x, y, c] = sums[c]
            return carry

        lax.fori_loop(0, 4, along_y, 0)
    for y, ey in ((0, -1), (3, 1)):
        for x in range(4):
            wide = load_wide(data_ref, x, y)
            here_z = [wide[2] - float(ez - 1) for ez in range(3)]
            sums = tuple(sums_ref[x, y, c] for c in range(4))
            for ex in (-1, 0, 1):
                if 0 <= x + ex < 4:
                    sums = pair_sums(
                        sums, wide[0] - float(ex), wide[1] - float(ey), here_z, x + ex + 1, y + ey + 1, table_ref
                    )
            for c in range(4):
                sums_ref[x, y, c] = sums[c]


def align_operators(whole_ref, aligned_ref):
    slot = 0
    for _, members in offset_groups():
        for index in members:
            begin = index * TERMS
            if begin + LANES <= whole_ref.shape[1]:
                piece = whole_ref[:, begin : begin + LANES]
            else:
                tail = whole_ref[:, begin : begin + TERMS]
                piece = jnp.concatenate([tail, jnp.zeros((TERMS, LANES - TERMS), BF16)], axis=1)
            aligned_ref[:TERMS, slot * LANES : (slot + 1) * LANES] = piece
            slot += 1


def gather_boxes(wide_ref, mids_ref, rows_ref):
    def step(n, carry):
        step_x, step_y, step_z = n // 9, n // 3 % 3, n % 3
        for octant in range(8):
            rows_ref[pl.ds(pl.multiple_of(n * 128 + octant * 16 + 8, 8), 8), :] = jnp.zeros((8, LANES), F32)
        for parent in range(8):
            px, py, pz = parent >> 2, parent >> 1 & 1, parent & 1
            rows_ref[pl.ds(n * 128 + parent, 8, stride=16), :] = wide_ref[px + step_x, py + step_y, pz + step_z]
        rows_ref[pl.ds(n * 128 + 8, 8, stride=16), :] = mids_ref[n]
        return carry

    lax.fori_loop(0, 27, step, 0)


def gather_upper(tops, tops_ref, rows_ref):
    def step(n, carry):
        step_x, step_y, step_z = n // 9, n // 3 % 3, n % 3
        far_x = lax.rem(tops[0] + step_x + 3, 4) * 2
        far_y = lax.rem(tops[1] + step_y + 1, 2) * 2
        far_z = lax.rem(tops[2] + step_z + 3, 4) * 2
        for octant in range(8):
            ox, oy, oz = octant >> 2, octant >> 1 & 1, octant & 1
            rows_ref[pl.ds(n * 128 + octant * 16 + 9, 1), :] = tops_ref[far_x + ox, far_y + oy, far_z + oz]
        return carry

    lax.fori_loop(0, 27, step, 0)


def convert_tiles(rows_ref, tiles_ref):
    def step(n, carry):
        for octant in range(8):
            start = pl.multiple_of(n * 128 + octant * 16, 16)
            tiles_ref[n * 8 + octant] = rows_ref[pl.ds(start, 16), :].astype(BF16)
        return carry

    lax.fori_loop(0, 27, step, 0)
    for tile in EXTRA_TILES.values():
        tiles_ref[tile] = rows_ref[tile * 16 : tile * 16 + 16, :].astype(BF16)


def gather_top(tops, tops_ref, upper_ref, operators, lattice_ref, turned_ref, rows_ref):
    for octant in range(8):
        ox, oy, oz = octant >> 2, octant >> 1 & 1, octant & 1
        for box in range(32):
            bx, by, bz = box >> 3, box >> 2 & 1, box & 3
            upper_ref[octant, box : box + 1, :] = tops_ref[2 * bx + ox, 2 * by + oy, 2 * bz + oz]
    coarse = jnp.zeros((32, TERMS), F32)
    for octant in range(8):
        coarse = coarse + split_nt(upper_ref[octant][:, :TERMS], operators[octant])
    lattice_term = split_nt(jnp.sum(coarse, axis=0, keepdims=True), lattice_ref[...])
    row = lax.broadcasted_iota(jnp.int32, (32, 32), 0)
    column = lax.broadcasted_iota(jnp.int32, (32, 32), 1)
    wanted = (
        (row // 8 + tops[0]) % 4 * 8 + (row // 4 % 2 + tops[1]) % 2 * 4 + (row % 4 + tops[2]) % 4
    )
    turned_ref[...] = jnp.dot(
        (wanted == column).astype(F32).astype(BF16), widen(coarse).astype(BF16), preferred_element_type=F32
    )
    for shift in offset_table():
        parity = top_parity(shift)
        source = shift[0] % 4 * 8 + shift[1] % 2 * 4 + shift[2] % 4
        if parity is not None:
            place = [shift[axis] + (parity >> (2 - axis) & 1) for axis in range(3)]
            target = tile_of(place) * 16 + TOP_ROWS[parity]
            rows_ref[target : target + 1, :] = turned_ref[source : source + 1, :]
        else:
            ((parity, place),) = admitted(shift)
            begin, target = tile_of(place) * 16, EXTRA_TILES[parity] * 16
            which = lax.broadcasted_iota(jnp.int32, (8, LANES), 0)
            lower = jnp.where(which < 2, rows_ref[begin + 8 : begin + 16, :], 0.0)
            top = jnp.broadcast_to(turned_ref[source : source + 1, :], (8, LANES))
            rows_ref[target : target + 8, :] = rows_ref[begin : begin + 8, :]
            rows_ref[target + 8 : target + 16, :] = jnp.where(which == 2, top, lower)
    return lattice_term


def far_products(tiles_ref, aligned_ref, acc_ref):
    total = [jnp.zeros((16, TERMS), F32) for _ in range(8)]
    extra = jnp.zeros((1, TERMS), F32)
    shifts = offset_table()
    slot = 0
    for parities, members in offset_groups():
        for start in range(0, len(members), CHUNK):
            part = members[start : start + CHUNK]
            special = len(parities) == 1 and parities[0] in EXTRA_TILES
            columns = []
            for index in part:
                tiles = [EXTRA_TILES[parities[0]]] if special else [tile_of(place) for _, place in admitted(shifts[index])]
                columns.append(jnp.concatenate([tiles_ref[tile] for tile in tiles], axis=0))
            data = columns[0] if len(columns) == 1 else jnp.concatenate(columns, axis=1)
            product = lanes_nt(data, aligned_ref[:TERMS, slot * LANES : (slot + len(part)) * LANES])
            slot += len(part)
            for place, parity in enumerate(parities):
                total[parity] = total[parity] + product[place * 16 : place * 16 + 16]
            if special:
                extra = extra + product[10:11]
    for parity in range(8):
        acc_ref[parity * 16 : parity * 16 + 16, :] = widen(total[parity])
    return extra


def locals_down(octant_own, acc_ref, lattice_term, down_rows, local_ref):
    own_down = jnp.where(
        lax.broadcasted_iota(jnp.int32, (TERMS * 8, LANES), 0) % 8 == octant_own, down_rows[...], 0.0
    )
    own_down = jnp.sum(own_down.reshape(TERMS, 8, LANES), axis=1)[:, :TERMS].astype(BF16)
    downs = [octant_operator(down_rows, octant) for octant in range(8)]
    far_top = lattice_term
    for parity, place in TOP_ROWS.items():
        row = parity * 16 + place
        far_top = far_top + acc_ref[row : row + 1, :][:, :TERMS]
    local_upper = 0.25 * acc_ref[pl.ds(octant_own * 16 + 9, 1), :][:, :TERMS] + split_nt(0.125 * far_top, own_down)
    upper_wide = jnp.broadcast_to(local_upper, (8, TERMS))
    which = lax.broadcasted_iota(jnp.int32, (8, TERMS), 0)
    local_mid = 0.5 * acc_ref[pl.ds(8, 8, stride=16), :][:, :TERMS]
    for octant in range(8):
        local_mid = local_mid + jnp.where(which == octant, split_nt(upper_wide, downs[octant]), 0.0)
    for octant in range(8):
        local = acc_ref[octant * 16 : octant * 16 + 8, :][:, :TERMS] + split_nt(local_mid, downs[octant])
        local_ref[octant * 8 : octant * 8 + 8, :] = widen(local)


def evaluate(local_ref, slope_ref, high_ref, low_ref, sums_ref, data_ref, live_ref, pot_ref, field_ref):
    local_leaf = local_ref[...]
    upper, lower = halves(local_leaf[:, :TERMS])
    slopes = jnp.dot(upper, slope_ref[...], preferred_element_type=F32) + jnp.dot(
        lower, slope_ref[...], preferred_element_type=F32
    )
    parts = [local_leaf] + [slopes[:, c * LANES : (c + 1) * LANES] for c in range(3)]
    split_parts = [halves(part[:, :KPAD]) for part in parts]
    row = lax.broadcasted_iota(jnp.int32, (16, LANES), 0)
    lane = lax.broadcasted_iota(jnp.int32, (16, LANES), 1)
    self_weight = lax.rsqrt(jnp.full((1, LANES), SOFTENING, F32))
    for parity in range(4):
        span = slice(parity * 16, parity * 16 + 16)
        coef_high = jnp.concatenate([part[0][span] for part in split_parts], axis=0)
        coef_low = jnp.concatenate([part[1][span] for part in split_parts], axis=0)
        coef = jnp.concatenate([coef_high, coef_low], axis=0)
        for group in range(4):
            x, y = (group >> 1) * 2 + (parity >> 1), (group & 1) * 2 + (parity & 1)
            tile = group * 4 + parity
            lanes = slice(tile * LANES, tile * LANES + LANES)
            both = jnp.dot(coef, high_ref[:, lanes], preferred_element_type=F32)
            value = both[:64] + both[64:] + jnp.dot(coef_high, low_ref[:, lanes], preferred_element_type=F32)
            hit = (row // 8 == lane // 32 % 2) & (row % 8 == group * 2 + lane // 64)
            sums = [
                jnp.sum(jnp.where(hit, value[16 * c : 16 * c + 16], 0.0), axis=0, keepdims=True) for c in range(4)
            ]
            near = [jnp.sum(sums_ref[x, y, c], axis=0, keepdims=True) for c in range(4)]
            live = live_ref[x, y : y + 1, :]
            near[0] = near[0] - data_ref[x, y, 3:4, :] * self_weight
            pot_ref[x, y : y + 1, :] = (near[0] + sums[0]) * live
            for c in range(3):
                field_ref[c, x, y : y + 1, :] = (near[c + 1] - sums[c + 1]) * live


def whole_kernel(
    nx,
    ny,
    nz,
    pos_ref,
    chg_ref,
    cnt_ref,
    exps_ref,
    slope_ref,
    up_ref,
    down_ref,
    lattice_ref,
    far_ref,
    pot_ref,
    field_ref,
    data_ref,
    live_ref,
    ext_ref,
    wide_ref,
    mids_ref,
    tops_ref,
    leaf_ref,
    mid_ref,
    top_ref,
    up_rows,
    down_rows,
    high_ref,
    low_ref,
    turned_ref,
    table_ref,
    sums_ref,
    whole_ref,
    aligned_ref,
    rows_ref,
    tiles_ref,
    upper_ref,
    coarse_ref,
    acc_ref,
    local_ref,
    send,
    recv,
    gsend,
    grecv,
    own,
):
    ix, iy, iz = lax.axis_index("gx"), lax.axis_index("gy"), lax.axis_index("gz")

    def at(dx, dy, dz):
        return {
            "gx": lax.rem(ix + (dx + nx), nx),
            "gy": lax.rem(iy + (dy + ny), ny),
            "gz": lax.rem(iz + (dz + nz), nz),
        }

    plane = [(0, b, c) for b in range(ny) for c in range(nz) if b or c]
    line = [(a, 0, 0) for a in range(1, nx)]
    wrapped = lambda step: (step[0] % nx, step[1] % ny, step[2] % nz)
    partners = sorted({wrapped(step) for step in DIRECTIONS} | set(plane) | set(line))
    barrier = pltpu.get_barrier_semaphore()
    for step in partners:
        pl.semaphore_signal(barrier, inc=1, device_id=at(*step), device_id_type=MESH)
    fetch = pltpu.make_async_copy(far_ref, whole_ref, own.at[4])
    fetch.start()

    prepare(pos_ref, chg_ref, cnt_ref, data_ref, live_ref)
    octant_operators(up_ref, up_rows)
    monomial_tiles(rows_from(data_ref), exps_ref, high_ref, low_ref)
    moments(data_ref, up_rows, leaf_ref, mid_ref, top_ref, high_ref, low_ref)

    pl.semaphore_wait(barrier, len(partners))

    def remote(src, dst, ssem, rsem, step):
        copy = pltpu.make_async_remote_copy(
            src_ref=src, dst_ref=dst, send_sem=ssem, recv_sem=rsem, device_id=at(*step), device_id_type=MESH
        )
        copy.start()
        return copy

    local = [
        pltpu.make_async_copy(data_ref, ext_ref.at[pl.ds(1, 4), pl.ds(1, 4), 1], own.at[0]),
        pltpu.make_async_copy(leaf_ref, wide_ref.at[pl.ds(1, 2), pl.ds(1, 2), pl.ds(1, 2)], own.at[1]),
        pltpu.make_async_copy(mid_ref, mids_ref.at[13], own.at[2]),
        pltpu.make_async_copy(top_ref, tops_ref.at[ix, iy, iz], own.at[3]),
    ]
    for copy in local:
        copy.start()
    halo = {}
    order = sorted(range(len(DIRECTIONS)), key=lambda i: sum(abs(d) for d in DIRECTIONS[i][:2]))
    for index in order:
        dx, dy, dz = DIRECTIONS[index]
        from_x, to_x = span_of(dx, 4, 1)
        from_y, to_y = span_of(dy, 4, 1)
        src, dst = data_ref.at[from_x, from_y], ext_ref.at[to_x, to_y, 1 - dz]
        halo[index] = remote(src, dst, send.at[0, index], recv.at[0, index], DIRECTIONS[index])
    first = [
        remote(top_ref, tops_ref.at[ix, iy, iz], gsend.at[k], grecv.at[k], step) for k, step in enumerate(plane)
    ]
    boxes = []
    for index, step in enumerate(DIRECTIONS):
        spans = [span_of(d, 2, 1) for d in step]
        src = leaf_ref.at[spans[0][0], spans[1][0], spans[2][0]]
        dst = wide_ref.at[spans[0][1], spans[1][1], spans[2][1]]
        boxes.append(remote(src, dst, send.at[1, index], recv.at[1, index], step))
        slot = ((1 - step[0]) * 3 + (1 - step[1])) * 3 + (1 - step[2])
        boxes.append(remote(mid_ref, mids_ref.at[slot], send.at[2, index], recv.at[2, index], step))

    octant_operators(down_ref, down_rows)
    fetch.wait()
    align_operators(whole_ref, aligned_ref)
    for copy in local:
        copy.wait()
    for index in order[:2]:
        halo[index].wait()
    inside = [(x, y) for x in range(1, 5) for y in range(1, 5)]
    fill_cells(inside, ext_ref, turned_ref, table_ref)
    near_inside((0, 1), data_ref, table_ref, sums_ref)
    for copy in first:
        copy.wait()
    second = [
        remote(tops_ref.at[ix], tops_ref.at[ix], gsend.at[32 + k], grecv.at[32 + k], step)
        for k, step in enumerate(line)
    ]
    near_inside((2, 3), data_ref, table_ref, sums_ref)
    for index in order[2:]:
        halo[index].wait()
    fill_cells(
        [(x, y) for x in range(6) for y in range(6) if (x, y) not in inside], ext_ref, turned_ref, table_ref
    )
    near_outside(data_ref, table_ref, sums_ref)
    for copy in boxes:
        copy.wait()
    gather_boxes(wide_ref, mids_ref, rows_ref)
    for copy in second:
        copy.wait()
    tops = (ix // 2, iy // 2, iz // 2)
    octant_own = (ix % 2) * 4 + (iy % 2) * 2 + iz % 2
    gather_upper(tops, tops_ref, rows_ref)
    operators = [octant_operator(up_rows, octant) for octant in range(8)]
    lattice_term = gather_top(tops, tops_ref, upper_ref, operators, lattice_ref, coarse_ref, rows_ref)
    convert_tiles(rows_ref, tiles_ref)
    extra = far_products(tiles_ref, aligned_ref, acc_ref)
    locals_down(octant_own, acc_ref, lattice_term + extra, down_rows, local_ref)
    evaluate(local_ref, slope_ref, high_ref, low_ref, sums_ref, data_ref, live_ref, pot_ref, field_ref)


VMEM = pl.BlockSpec(memory_space=pltpu.VMEM)


def shape(*dims):
    return jax.ShapeDtypeStruct(dims, F32)


def whole_call(sizes, *operands):
    dma = pltpu.SemaphoreType.DMA
    return pl.pallas_call(
        functools.partial(whole_kernel, *sizes),
        out_shape=(shape(4, 4, LANES), shape(3, 4, 4, LANES)),
        in_specs=[VMEM] * 8 + [pl.BlockSpec(memory_space=pl.ANY)],
        out_specs=(VMEM,) * 2,
        scratch_shapes=[
            pltpu.VMEM((4, 4, 4, LANES), F32),
            pltpu.VMEM((4, 4, LANES), F32),
            pltpu.VMEM((6, 6, 3, 4, LANES), F32),
            pltpu.VMEM((4, 4, 4, 8, LANES), F32),
            pltpu.VMEM((27, 8, LANES), F32),
            pltpu.VMEM((*sizes, 1, LANES), F32),
            pltpu.VMEM((2, 2, 2, 8, LANES), F32),
            pltpu.VMEM((8, LANES), F32),
            pltpu.VMEM((1, LANES), F32),
            pltpu.VMEM((TERMS * 8, LANES), F32),
            pltpu.VMEM((TERMS * 8, LANES), F32),
            pltpu.VMEM((KPAD, 2048), BF16),
            pltpu.VMEM((KPAD, 2048), BF16),
            pltpu.VMEM((6, 6, 3, 4, LANES), F32),
            pltpu.VMEM((6, 6, 3, 4, SLOTS, LANES), F32),
            pltpu.VMEM((4, 4, 4, 8, LANES), F32),
            pltpu.VMEM((TERMS, 25600), BF16),
            pltpu.VMEM((KPAD, OFFSETS * LANES), BF16),
            pltpu.VMEM((218 * 16, LANES), F32),
            pltpu.VMEM((218, 16, LANES), BF16),
            pltpu.VMEM((8, 32, LANES), F32),
            pltpu.VMEM((32, LANES), F32),
            pltpu.VMEM((LANES, LANES), F32),
            pltpu.VMEM((64, LANES), F32),
            dma((3, 26)),
            dma((3, 26)),
            dma((40,)),
            dma((40,)),
            dma((5,)),
        ],
        compiler_params=pltpu.CompilerParams(collective_id=0, has_side_effects=True),
        name="whole",
    )(*operands)


def solution(mesh):
    sizes = tuple(mesh.shape[axis] for axis in ("gx", "gy", "gz"))

    def per_device(
        positions, charges, counts, moment_shift, far_operators, local_shift, lattice_operator
    ):
        exps = jnp.asarray(exponent_planes())
        slope = jnp.asarray(slope_matrix()).astype(BF16)
        native_up = jnp.transpose(moment_shift, (1, 0, 2))
        native_down = jnp.transpose(local_shift, (1, 0, 2))
        return whole_call(
            sizes,
            positions,
            charges,
            counts,
            exps,
            slope,
            native_up,
            native_down,
            lattice_operator,
            far_operators,
        )

    placed = (
        P(None, "gx", "gy", "gz"),
        P("gx", "gy", "gz"),
        P("gx", "gy", "gz"),
        P(),
        P(),
        P(),
        P(),
    )
    return jax.shard_map(
        per_device,
        mesh=mesh,
        in_specs=placed,
        out_specs=(P("gx", "gy", "gz"), P(None, "gx", "gy", "gz")),
        check_vma=False,
    )
```

time: 51.9 us -> 38.3 us (0.74)
  Pallas kernels: 51.1 us -> 34.8 us
  local copies, waits for them, and re-layouts: 0 us -> 2.64 us
    pallas_call x2 -> x1, Pallas kernels: 51.1 us -> 34.8 us  [whole_call(): pl.pallas_call(functools.partial(whole_kernel, *sizes), out_shape=(shape(...]
    unnamed x0 -> x2, local copies, waits for them, and re-layouts: none -> 2.64 us
where the time goes in v2:
time: 38.3 us; the launch traced here: 38.1 us
  Pallas kernels  34.8 us (91%)
  local copies, waits for them, and re-layouts  2.64 us (7%)
  between operations  0.64 us (2%)
    pallas_call x1, Pallas kernels, whole_call(): pl.pallas_call(functools.partial(whole_kernel, *sizes), out_shape=(shape(...  34.8 us
    unnamed x2, local copies, waits for them, and re-layouts  2.64 us

profile of v2, /device:TPU:1, one launch (start us, length us, event | category | flops | bytes accessed | tf_op | source)
XLA Modules:
  0.0 38.1 jit_solution(14110052815438365775)
XLA Ops:
  0.6 34.8 %whole.1 = (f32[4,4,128]{2,1,0:T(4,128)}, f32[3,4,4,128]{3,2,1,0:T(4,128)}) custom-call(f32[3,4,4,128]{3,2,1,0:T(4,128)} %pos_ref.1, f32[4,4,128]{2,1,0:T(4,128)} %chg_ref.1, s32[4,4,4]{2,1,0:T(4,128)} %cnt_ref.1, s32[4,96,128]{2,1,0:T(8,128)} %constant.4.clone.exps_ref, bf16[81,384]{1,0:T(8,128)(2,1)} %constant.9.slope_ref, bf16[81,8,81]{2,1,0:T(8,128)(2,1)} %bitcast.2, ...), custom_call_target="tpu_custom_call" | custom-call | tf_op jit(solution)/shard_map/whole/pallas_call | solution.py:642
  35.4 1.3 %copy.13 = f32[4,4,128]{2,1,0:T(4,128)} copy(f32[4,4,128]{2,1,0:T(4,128)} %get-tuple-element.4) | data formatting | bytes 16384
  36.7 1.3 %copy.14 = f32[3,4,4,128]{3,2,1,0:T(4,128)} copy(f32[3,4,4,128]{3,2,1,0:T(4,128)} %get-tuple-element.5) | data formatting | bytes 49152

commit v3 on v2

--- a/solution.py
+++ b/solution.py
@@ -16,6 +16,7 @@
 LANES = 128
 OFFSETS = 316
 CHUNK = 4
+PIECES = 4
 MESH = pl.DeviceIdType.MESH
 F32 = jnp.float32
 BF16 = jnp.bfloat16
@@ -73,13 +74,6 @@
             for power_x in range(accumulated - height + 1):
                 listed.append((power_x, accumulated - height - power_x, height))
     return listed
-
-
-def exponent_planes():
-    planes = np.zeros((4, KPAD, LANES), np.int32)
-    for row, (a, b, c) in enumerate(exponent_list()):
-        planes[0, row], planes[1, row], planes[2, row], planes[3, row] = a, b, c, 1
-    return planes
 
 
 def slope_matrix():
@@ -109,9 +103,9 @@
     rows = value.shape[0]
     if rows % 8:
         value = jnp.concatenate([value, jnp.zeros((8 - rows, value.shape[1]), F32)], axis=0)
-    upper, lower = halves(value)
-    both = lanes_nt(upper, rhs) + lanes_nt(lower, rhs)
-    return both[:rows]
+    size = value.shape[0]
+    both = lanes_nt(jnp.concatenate(halves(value), axis=0), rhs)
+    return (both[:size] + both[size:])[:rows]
 
 
 def widen(value):
@@ -128,14 +122,26 @@
     return jnp.where(exponents == 8, eighth, result)
 
 
-def monomial_tiles(rows_of, exps_ref, high_ref, low_ref):
+def exponents():
+    row = lax.broadcasted_iota(jnp.int32, (KPAD, LANES), 0)
+    degree = jnp.zeros((KPAD, LANES), jnp.int32)
+    for n in range(1, ORDER + 1):
+        degree = degree + (row >= n * n).astype(jnp.int32)
+    place = row - degree * degree
+    height = (place > degree).astype(jnp.int32)
+    power_x = place - height * (degree + 1)
+    return power_x, degree - height - power_x, height, row < TERMS
+
+
+def monomial_tiles(rows_of, high_ref, low_ref):
+    power_x, power_y, power_z, valid = exponents()
     for tile in range(16):
         px, py, ox, oy = tile >> 3, tile >> 2 & 1, tile >> 1 & 1, tile & 1
         row_x, row_y, row_z = rows_of(2 * px + ox, 2 * py + oy)
         full = lambda row: jnp.broadcast_to(row - 0.5, (KPAD, LANES))
-        value = power_of(full(row_x), exps_ref[0]) * power_of(full(row_y), exps_ref[1])
-        value = value * jnp.where(exps_ref[2] != 0, full(row_z), 1.0)
-        value = jnp.where(exps_ref[3] != 0, value, 0.0)
+        value = power_of(full(row_x), power_x) * power_of(full(row_y), power_y)
+        value = value * jnp.where(power_z != 0, full(row_z), 1.0)
+        value = jnp.where(valid, value, 0.0)
         upper, lower = halves(value)
         high_ref[:, tile * LANES : (tile + 1) * LANES] = upper
         low_ref[:, tile * LANES : (tile + 1) * LANES] = lower
@@ -315,57 +321,54 @@
                 sums_ref[x, y, c] = sums[c]
 
 
-def align_operators(whole_ref, aligned_ref):
-    slot = 0
+def align_operators(first, last, whole_ref, aligned_ref):
+    slots = {}
     for _, members in offset_groups():
         for index in members:
-            begin = index * TERMS
-            if begin + LANES <= whole_ref.shape[1]:
-                piece = whole_ref[:, begin : begin + LANES]
-            else:
-                tail = whole_ref[:, begin : begin + TERMS]
-                piece = jnp.concatenate([tail, jnp.zeros((TERMS, LANES - TERMS), BF16)], axis=1)
-            aligned_ref[:TERMS, slot * LANES : (slot + 1) * LANES] = piece
-            slot += 1
-
-
-def gather_boxes(wide_ref, mids_ref, rows_ref):
+            slots[index] = len(slots)
+    for index in range(first, last):
+        begin = index * TERMS
+        if begin + LANES <= whole_ref.shape[1]:
+            piece = whole_ref[:, begin : begin + LANES]
+        else:
+            tail = whole_ref[:, begin : begin + TERMS]
+            piece = jnp.concatenate([tail, jnp.zeros((TERMS, LANES - TERMS), BF16)], axis=1)
+        slot = slots[index]
+        aligned_ref[:TERMS, slot * LANES : (slot + 1) * LANES] = piece
+
+
+def clear_rows(rows_ref):
     def step(n, carry):
-        step_x, step_y, step_z = n // 9, n // 3 % 3, n % 3
         for octant in range(8):
             rows_ref[pl.ds(pl.multiple_of(n * 128 + octant * 16 + 8, 8), 8), :] = jnp.zeros((8, LANES), F32)
+        return carry
+
+    lax.fori_loop(0, 27, step, 0)
+
+
+def gather_boxes(wide_ref, mids_ref, rows_ref):
+    for n in range(27):
+        step_x, step_y, step_z = n // 9, n // 3 % 3, n % 3
         for parent in range(8):
             px, py, pz = parent >> 2, parent >> 1 & 1, parent & 1
             rows_ref[pl.ds(n * 128 + parent, 8, stride=16), :] = wide_ref[px + step_x, py + step_y, pz + step_z]
         rows_ref[pl.ds(n * 128 + 8, 8, stride=16), :] = mids_ref[n]
-        return carry
-
-    lax.fori_loop(0, 27, step, 0)
 
 
 def gather_upper(tops, tops_ref, rows_ref):
-    def step(n, carry):
+    far_x = [lax.rem(tops[0] + step + 3, 4) * 2 for step in range(3)]
+    far_y = [lax.rem(tops[1] + step + 1, 2) * 2 for step in range(3)]
+    far_z = [lax.rem(tops[2] + step + 3, 4) * 2 for step in range(3)]
+    for n in range(27):
         step_x, step_y, step_z = n // 9, n // 3 % 3, n % 3
-        far_x = lax.rem(tops[0] + step_x + 3, 4) * 2
-        far_y = lax.rem(tops[1] + step_y + 1, 2) * 2
-        far_z = lax.rem(tops[2] + step_z + 3, 4) * 2
         for octant in range(8):
             ox, oy, oz = octant >> 2, octant >> 1 & 1, octant & 1
-            rows_ref[pl.ds(n * 128 + octant * 16 + 9, 1), :] = tops_ref[far_x + ox, far_y + oy, far_z + oz]
-        return carry
-
-    lax.fori_loop(0, 27, step, 0)
+            place = n * 128 + octant * 16 + 9
+            rows_ref[place : place + 1, :] = tops_ref[far_x[step_x] + ox, far_y[step_y] + oy, far_z[step_z] + oz]
 
 
 def convert_tiles(rows_ref, tiles_ref):
-    def step(n, carry):
-        for octant in range(8):
-            start = pl.multiple_of(n * 128 + octant * 16, 16)
-            tiles_ref[n * 8 + octant] = rows_ref[pl.ds(start, 16), :].astype(BF16)
-        return carry
-
-    lax.fori_loop(0, 27, step, 0)
-    for tile in EXTRA_TILES.values():
+    for tile in range(218):
         tiles_ref[tile] = rows_ref[tile * 16 : tile * 16 + 16, :].astype(BF16)
 
 
@@ -430,24 +433,31 @@
     return extra
 
 
-def locals_down(octant_own, acc_ref, lattice_term, down_rows, local_ref):
-    own_down = jnp.where(
+def down_operators(octant_own, down_rows, downs_ref):
+    own = jnp.where(
         lax.broadcasted_iota(jnp.int32, (TERMS * 8, LANES), 0) % 8 == octant_own, down_rows[...], 0.0
     )
-    own_down = jnp.sum(own_down.reshape(TERMS, 8, LANES), axis=1)[:, :TERMS].astype(BF16)
-    downs = [octant_operator(down_rows, octant) for octant in range(8)]
+    downs_ref[8, :TERMS, :] = jnp.sum(own.reshape(TERMS, 8, LANES), axis=1).astype(BF16)
+    for octant in range(8):
+        downs_ref[octant, :TERMS, :TERMS] = octant_operator(down_rows, octant)
+
+
+def locals_down(octant_own, acc_ref, lattice_term, downs_ref, local_ref):
     far_top = lattice_term
     for parity, place in TOP_ROWS.items():
         row = parity * 16 + place
         far_top = far_top + acc_ref[row : row + 1, :][:, :TERMS]
-    local_upper = 0.25 * acc_ref[pl.ds(octant_own * 16 + 9, 1), :][:, :TERMS] + split_nt(0.125 * far_top, own_down)
+    operator = lambda octant: downs_ref[octant, :TERMS, :TERMS]
+    local_upper = 0.25 * acc_ref[pl.ds(octant_own * 16 + 9, 1), :][:, :TERMS] + split_nt(
+        0.125 * far_top, operator(8)
+    )
     upper_wide = jnp.broadcast_to(local_upper, (8, TERMS))
     which = lax.broadcasted_iota(jnp.int32, (8, TERMS), 0)
     local_mid = 0.5 * acc_ref[pl.ds(8, 8, stride=16), :][:, :TERMS]
     for octant in range(8):
-        local_mid = local_mid + jnp.where(which == octant, split_nt(upper_wide, downs[octant]), 0.0)
+        local_mid = local_mid + jnp.where(which == octant, split_nt(upper_wide, operator(octant)), 0.0)
     for octant in range(8):
-        local = acc_ref[octant * 16 : octant * 16 + 8, :][:, :TERMS] + split_nt(local_mid, downs[octant])
+        local = acc_ref[octant * 16 : octant * 16 + 8, :][:, :TERMS] + split_nt(local_mid, operator(octant))
         local_ref[octant * 8 : octant * 8 + 8, :] = widen(local)
 
 
@@ -489,17 +499,23 @@
     nx,
     ny,
     nz,
+    pos_hbm,
+    chg_hbm,
+    cnt_hbm,
+    up_hbm,
+    down_hbm,
+    slope_hbm,
+    lattice_hbm,
+    far_hbm,
+    pot_ref,
+    field_ref,
     pos_ref,
     chg_ref,
     cnt_ref,
-    exps_ref,
-    slope_ref,
     up_ref,
     down_ref,
+    slope_ref,
     lattice_ref,
-    far_ref,
-    pot_ref,
-    field_ref,
     data_ref,
     live_ref,
     ext_ref,
@@ -511,6 +527,7 @@
     top_ref,
     up_rows,
     down_rows,
+    downs_ref,
     high_ref,
     low_ref,
     turned_ref,
@@ -529,6 +546,7 @@
     gsend,
     grecv,
     own,
+    load,
 ):
     ix, iy, iz = lax.axis_index("gx"), lax.axis_index("gy"), lax.axis_index("gz")
 
@@ -546,12 +564,22 @@
     barrier = pltpu.get_barrier_semaphore()
     for step in partners:
         pl.semaphore_signal(barrier, inc=1, device_id=at(*step), device_id_type=MESH)
-    fetch = pltpu.make_async_copy(far_ref, whole_ref, own.at[4])
-    fetch.start()
+    operands = ((pos_hbm, pos_ref), (chg_hbm, chg_ref), (cnt_hbm, cnt_ref), (up_hbm, up_ref))
+    operands += ((down_hbm, down_ref), (slope_hbm, slope_ref), (lattice_hbm, lattice_ref))
+    loads = [pltpu.make_async_copy(src, dst, load.at[k]) for k, (src, dst) in enumerate(operands)]
+    pieces = []
+    for k in range(PIECES):
+        span = pl.ds(k * (25600 // PIECES), 25600 // PIECES)
+        pieces.append(pltpu.make_async_copy(far_hbm.at[:, span], whole_ref.at[:, span], load.at[7 + k]))
+    for copy in loads + pieces:
+        copy.start()
+    octant_own = (ix % 2) * 4 + (iy % 2) * 2 + iz % 2
+    for copy in loads[:4]:
+        copy.wait()
 
     prepare(pos_ref, chg_ref, cnt_ref, data_ref, live_ref)
     octant_operators(up_ref, up_rows)
-    monomial_tiles(rows_from(data_ref), exps_ref, high_ref, low_ref)
+    monomial_tiles(rows_from(data_ref), high_ref, low_ref)
     moments(data_ref, up_rows, leaf_ref, mid_ref, top_ref, high_ref, low_ref)
 
     pl.semaphore_wait(barrier, len(partners))
@@ -591,9 +619,17 @@
         slot = ((1 - step[0]) * 3 + (1 - step[1])) * 3 + (1 - step[2])
         boxes.append(remote(mid_ref, mids_ref.at[slot], send.at[2, index], recv.at[2, index], step))
 
+    for copy in loads[4:]:
+        copy.wait()
     octant_operators(down_ref, down_rows)
-    fetch.wait()
-    align_operators(whole_ref, aligned_ref)
+    down_operators(octant_own, down_rows, downs_ref)
+    clear_rows(rows_ref)
+    done = 0
+    for k in range(PIECES):
+        pieces[k].wait()
+        ready = OFFSETS if k == PIECES - 1 else ((k + 1) * (25600 // PIECES) - LANES) // TERMS
+        align_operators(done, ready, whole_ref, aligned_ref)
+        done = ready
     for copy in local:
         copy.wait()
     for index in order[:2]:
@@ -620,13 +656,12 @@
     for copy in second:
         copy.wait()
     tops = (ix // 2, iy // 2, iz // 2)
-    octant_own = (ix % 2) * 4 + (iy % 2) * 2 + iz % 2
     gather_upper(tops, tops_ref, rows_ref)
     operators = [octant_operator(up_rows, octant) for octant in range(8)]
     lattice_term = gather_top(tops, tops_ref, upper_ref, operators, lattice_ref, coarse_ref, rows_ref)
     convert_tiles(rows_ref, tiles_ref)
     extra = far_products(tiles_ref, aligned_ref, acc_ref)
-    locals_down(octant_own, acc_ref, lattice_term + extra, down_rows, local_ref)
+    locals_down(octant_own, acc_ref, lattice_term + extra, downs_ref, local_ref)
     evaluate(local_ref, slope_ref, high_ref, low_ref, sums_ref, data_ref, live_ref, pot_ref, field_ref)
 
 
@@ -642,9 +677,16 @@
     return pl.pallas_call(
         functools.partial(whole_kernel, *sizes),
         out_shape=(shape(4, 4, LANES), shape(3, 4, 4, LANES)),
-        in_specs=[VMEM] * 8 + [pl.BlockSpec(memory_space=pl.ANY)],
+        in_specs=[pl.BlockSpec(memory_space=pltpu.HBM)] * 8,
         out_specs=(VMEM,) * 2,
         scratch_shapes=[
+            pltpu.VMEM((3, 4, 4, LANES), F32),
+            pltpu.VMEM((4, 4, LANES), F32),
+            pltpu.VMEM((4, 4, 4), jnp.int32),
+            pltpu.VMEM((TERMS, 8, TERMS), BF16),
+            pltpu.VMEM((TERMS, 8, TERMS), BF16),
+            pltpu.VMEM((TERMS, 3 * LANES), BF16),
+            pltpu.VMEM((TERMS, TERMS), BF16),
             pltpu.VMEM((4, 4, 4, LANES), F32),
             pltpu.VMEM((4, 4, LANES), F32),
             pltpu.VMEM((6, 6, 3, 4, LANES), F32),
@@ -656,6 +698,7 @@
             pltpu.VMEM((1, LANES), F32),
             pltpu.VMEM((TERMS * 8, LANES), F32),
             pltpu.VMEM((TERMS * 8, LANES), F32),
+            pltpu.VMEM((9, KPAD, LANES), BF16),
             pltpu.VMEM((KPAD, 2048), BF16),
             pltpu.VMEM((KPAD, 2048), BF16),
             pltpu.VMEM((6, 6, 3, 4, LANES), F32),
@@ -673,9 +716,12 @@
             dma((3, 26)),
             dma((40,)),
             dma((40,)),
-            dma((5,)),
+            dma((4,)),
+            dma((7 + PIECES,)),
         ],
-        compiler_params=pltpu.CompilerParams(collective_id=0, has_side_effects=True),
+        compiler_params=pltpu.CompilerParams(
+            collective_id=0, has_side_effects=True, vmem_limit_bytes=56000000
+        ),
         name="whole",
     )(*operands)
 
@@ -686,7 +732,6 @@
     def per_device(
         positions, charges, counts, moment_shift, far_operators, local_shift, lattice_operator
     ):
-        exps = jnp.asarray(exponent_planes())
         slope = jnp.asarray(slope_matrix()).astype(BF16)
         native_up = jnp.transpose(moment_shift, (1, 0, 2))
         native_down = jnp.transpose(local_shift, (1, 0, 2))
@@ -695,10 +740,9 @@
             positions,
             charges,
             counts,
-            exps,
-            slope,
             native_up,
             native_down,
+            slope,
             lattice_operator,
             far_operators,
         )

time: 38.3 us -> 39.4 us (1.029)
  local copies, waits for them, and re-layouts: 2.64 us -> 6.78 us
  Pallas kernels: 34.8 us -> 31.6 us
    unnamed x2 -> x16, local copies, waits for them, and re-layouts: 2.64 us -> 6.78 us
    pallas_call x1, Pallas kernels: 34.8 us -> 31.6 us  [whole_call(): pl.pallas_call(functools.partial(whole_kernel, *sizes), out_shape=(shape(...]
where the time goes in v3:
time: 39.4 us; the launch traced here: 39 us
  Pallas kernels  31.6 us (80%)
  local copies, waits for them, and re-layouts  6.78 us (17%)
  between operations  0.66 us (2%)
    pallas_call x1, Pallas kernels, whole_call(): pl.pallas_call(functools.partial(whole_kernel, *sizes), out_shape=(shape(...  31.6 us
    unnamed x16, local copies, waits for them, and re-layouts  6.78 us

profile of v3, /device:TPU:1, one launch (start us, length us, event | category | flops | bytes accessed | tf_op | source)
XLA Modules:
  0.0 39.0 jit_solution(12344484966529131046)
XLA Ops:
  0.6 0.0 copy-start
  0.6 0.9 %copy-done = bf16[8,81,81]{2,0,1:T(8,128)(2,1)S(1)} copy-done((bf16[8,81,81]{2,0,1:T(8,128)(2,1)S(1)}, bf16[8,81,81]{2,0,1:T(8,128)(2,1)}, u32[]{:S(2)}) %copy-start) | copy-done | bytes 105000
  1.5 0.0 copy-start.1
  1.6 0.9 %copy-done.1 = bf16[8,81,81]{2,0,1:T(8,128)(2,1)S(1)} copy-done((bf16[8,81,81]{2,0,1:T(8,128)(2,1)S(1)}, bf16[8,81,81]{2,0,1:T(8,128)(2,1)}, u32[]{:S(2)}) %copy-start.1) | copy-done | bytes 105000
  2.5 0.0 copy-start.2
  2.5 0.9 %copy-done.2 = bf16[81,384]{1,0:T(8,128)(2,1)S(1)} copy-done((bf16[81,384]{1,0:T(8,128)(2,1)S(1)}, bf16[81,384]{1,0:T(8,128)(2,1)}, u32[]{:S(2)}) %copy-start.2) | copy-done | bytes 62232
  3.3 0.0 copy-start.3
  3.4 0.7 %copy-done.3 = f32[3,4,4,128]{3,2,1,0:T(4,128)S(1)} copy-done((f32[3,4,4,128]{3,2,1,0:T(4,128)S(1)}, f32[3,4,4,128]{3,2,1,0:T(4,128)}, u32[]{:S(2)}) %copy-start.3) | copy-done | bytes 24600
  4.1 0.0 copy-start.4
  4.1 0.7 %copy-done.4 = bf16[81,81]{1,0:T(8,128)(2,1)S(1)} copy-done((bf16[81,81]{1,0:T(8,128)(2,1)S(1)}, bf16[81,81]{1,0:T(8,128)(2,1)}, u32[]{:S(2)}) %copy-start.4) | copy-done | bytes 13146
  4.8 0.0 copy-start.5
  4.8 0.7 %copy-done.5 = f32[4,4,128]{2,1,0:T(4,128)S(1)} copy-done((f32[4,4,128]{2,1,0:T(4,128)S(1)}, f32[4,4,128]{2,1,0:T(4,128)}, u32[]{:S(2)}) %copy-start.5) | copy-done | bytes 8216
  5.5 0.0 copy-start.6
  5.5 0.7 %copy-done.6 = s32[4,4,4]{2,1,0:T(4,128)S(1)} copy-done((s32[4,4,4]{2,1,0:T(4,128)S(1)}, s32[4,4,4]{2,1,0:T(4,128)}, u32[]{:S(2)}) %copy-start.6) | copy-done | bytes 280
  6.2 31.6 %whole.1 = (f32[4,4,128]{2,1,0:T(4,128)S(1)}, f32[3,4,4,128]{3,2,1,0:T(4,128)S(1)}) custom-call(f32[3,4,4,128]{3,2,1,0:T(4,128)S(1)} %copy-done.3, f32[4,4,128]{2,1,0:T(4,128)S(1)} %copy-done.5, s32[4,4,4]{2,1,0:T(4,128)S(1)} %copy-done.6, bf16[81,8,81]{2,1,0:T(8,128)(2,1)S(1)} %bitcast.2, bf16[81,8,81]{2,1,0:T(8,128)(2,1)S(1)} %bitcast.3, ...), custom_call_target="tpu_custom_call" | custom-call | tf_op jit(solution)/shard_map/whole/pallas_call | solution.py:677
  37.8 0.6 %copy.12 = f32[4,4,128]{2,1,0:T(4,128)} copy(f32[4,4,128]{2,1,0:T(4,128)S(1)} %get-tuple-element.4) | data formatting | bytes 16384
  38.4 0.6 %copy.13 = f32[3,4,4,128]{3,2,1,0:T(4,128)} copy(f32[3,4,4,128]{3,2,1,0:T(4,128)S(1)} %get-tuple-element.5) | data formatting | bytes 49152
Async XLA Ops:
  0.6 0.9 %copy-start = (bf16[8,81,81]{2,0,1:T(8,128)(2,1)S(1)}, bf16[8,81,81]{2,0,1:T(8,128)(2,1)}, u32[]{:S(2)}) copy-start(bf16[8,81,81]{2,0,1:T(8,128)(2,1)} %param.11) | copy-start | bytes 314932
  1.5 0.9 %copy-start.1 = (bf16[8,81,81]{2,0,1:T(8,128)(2,1)S(1)}, bf16[8,81,81]{2,0,1:T(8,128)(2,1)}, u32[]{:S(2)}) copy-start(bf16[8,81,81]{2,0,1:T(8,128)(2,1)} %param.13) | copy-start | bytes 314932
  2.5 0.9 %copy-start.2 = (bf16[81,384]{1,0:T(8,128)(2,1)S(1)}, bf16[81,384]{1,0:T(8,128)(2,1)}, u32[]{:S(2)}) copy-start(bf16[81,384]{1,0:T(8,128)(2,1)} %constant.6.slope_hbm) | copy-start | bytes 186628
  3.3 0.7 %copy-start.3 = (f32[3,4,4,128]{3,2,1,0:T(4,128)S(1)}, f32[3,4,4,128]{3,2,1,0:T(4,128)}, u32[]{:S(2)}) copy-start(f32[3,4,4,128]{3,2,1,0:T(4,128)} %pos_hbm.1) | copy-start | bytes 73732
  4.1 0.7 %copy-start.4 = (bf16[81,81]{1,0:T(8,128)(2,1)S(1)}, bf16[81,81]{1,0:T(8,128)(2,1)}, u32[]{:S(2)}) copy-start(bf16[81,81]{1,0:T(8,128)(2,1)} %lattice_hbm.1) | copy-start | bytes 39370
  4.8 0.7 %copy-start.5 = (f32[4,4,128]{2,1,0:T(4,128)S(1)}, f32[4,4,128]{2,1,0:T(4,128)}, u32[]{:S(2)}) copy-start(f32[4,4,128]{2,1,0:T(4,128)} %chg_hbm.1) | copy-start | bytes 24580
  5.5 0.7 %copy-start.6 = (s32[4,4,4]{2,1,0:T(4,128)S(1)}, s32[4,4,4]{2,1,0:T(4,128)}, u32[]{:S(2)}) copy-start(s32[4,4,4]{2,1,0:T(4,128)} %cnt_hbm.1) | copy-start | bytes 772

commit v4 on v3

--- a/solution.py
+++ b/solution.py
@@ -461,7 +461,7 @@
         local_ref[octant * 8 : octant * 8 + 8, :] = widen(local)
 
 
-def evaluate(local_ref, slope_ref, high_ref, low_ref, sums_ref, data_ref, live_ref, pot_ref, field_ref):
+def evaluate(local_ref, slope_ref, high_ref, low_ref, sums_ref, data_ref, live_ref, out_ref):
     local_leaf = local_ref[...]
     upper, lower = halves(local_leaf[:, :TERMS])
     slopes = jnp.dot(upper, slope_ref[...], preferred_element_type=F32) + jnp.dot(
@@ -490,9 +490,9 @@
             near = [jnp.sum(sums_ref[x, y, c], axis=0, keepdims=True) for c in range(4)]
             live = live_ref[x, y : y + 1, :]
             near[0] = near[0] - data_ref[x, y, 3:4, :] * self_weight
-            pot_ref[x, y : y + 1, :] = (near[0] + sums[0]) * live
-            for c in range(3):
-                field_ref[c, x, y : y + 1, :] = (near[c + 1] - sums[c + 1]) * live
+            for c in range(4):
+                value = near[c] + sums[c] if c == 0 else near[c] - sums[c]
+                out_ref[c, x, y : y + 1, :] = value * live
 
 
 def whole_kernel(
@@ -507,8 +507,7 @@
     slope_hbm,
     lattice_hbm,
     far_hbm,
-    pot_ref,
-    field_ref,
+    out_ref,
     pos_ref,
     chg_ref,
     cnt_ref,
@@ -662,7 +661,7 @@
     convert_tiles(rows_ref, tiles_ref)
     extra = far_products(tiles_ref, aligned_ref, acc_ref)
     locals_down(octant_own, acc_ref, lattice_term + extra, downs_ref, local_ref)
-    evaluate(local_ref, slope_ref, high_ref, low_ref, sums_ref, data_ref, live_ref, pot_ref, field_ref)
+    evaluate(local_ref, slope_ref, high_ref, low_ref, sums_ref, data_ref, live_ref, out_ref)
 
 
 VMEM = pl.BlockSpec(memory_space=pltpu.VMEM)
@@ -676,9 +675,9 @@
     dma = pltpu.SemaphoreType.DMA
     return pl.pallas_call(
         functools.partial(whole_kernel, *sizes),
-        out_shape=(shape(4, 4, LANES), shape(3, 4, 4, LANES)),
+        out_shape=shape(4, 4, 4, LANES),
         in_specs=[pl.BlockSpec(memory_space=pltpu.HBM)] * 8,
-        out_specs=(VMEM,) * 2,
+        out_specs=VMEM,
         scratch_shapes=[
             pltpu.VMEM((3, 4, 4, LANES), F32),
             pltpu.VMEM((4, 4, LANES), F32),
@@ -719,11 +718,24 @@
             dma((4,)),
             dma((7 + PIECES,)),
         ],
-        compiler_params=pltpu.CompilerParams(
-            collective_id=0, has_side_effects=True, vmem_limit_bytes=56000000
-        ),
+        compiler_params=pltpu.CompilerParams(collective_id=0, has_side_effects=True),
         name="whole",
     )(*operands)
+
+
+def part_kernel(both_ref, pot_ref, field_ref):
+    pot_ref[...] = both_ref[0]
+    field_ref[...] = both_ref[1:4]
+
+
+def part_call(both):
+    return pl.pallas_call(
+        part_kernel,
+        out_shape=(shape(4, 4, LANES), shape(3, 4, 4, LANES)),
+        in_specs=[VMEM],
+        out_specs=(VMEM,) * 2,
+        name="part",
+    )(both)
 
 
 def solution(mesh):
@@ -735,7 +747,7 @@
         slope = jnp.asarray(slope_matrix()).astype(BF16)
         native_up = jnp.transpose(moment_shift, (1, 0, 2))
         native_down = jnp.transpose(local_shift, (1, 0, 2))
-        return whole_call(
+        both = whole_call(
             sizes,
             positions,
             charges,
@@ -746,6 +758,7 @@
             lattice_operator,
             far_operators,
         )
+        return part_call(both)
 
     placed = (
         P(None, "gx", "gy", "gz"),

time: 39.4 us -> 34.6 us (0.88)
  local copies, waits for them, and re-layouts: 6.78 us -> 0 us
  Pallas kernels: 31.6 us -> 33.8 us
    unnamed x16 -> x0, local copies, waits for them, and re-layouts: 6.78 us -> none
    pallas_call x1 -> x2, Pallas kernels: 31.6 us -> 33.8 us  [the longest x1 32.4 us: whole_call(): pl.pallas_call(functools.partial(whole_kernel, *sizes), out_shape=shape(4...]
where the time goes in v4:
time: 34.6 us; the launch traced here: 34.5 us
  Pallas kernels  33.8 us (98%)
  between operations  0.64 us (2%)
    pallas_call x1, Pallas kernels, whole_call(): pl.pallas_call(functools.partial(whole_kernel, *sizes), out_shape=shape(4...  32.4 us
    pallas_call x1, Pallas kernels, part_call(): pl.pallas_call(part_kernel, out_shape=(shape(4, 4, LANES), shape(3, 4, 4,...  1.37 us

profile of v4, /device:TPU:1, one launch (start us, length us, event | category | flops | bytes accessed | tf_op | source)
XLA Modules:
  0.0 34.5 jit_solution(17607709643601679931)
XLA Ops:
  0.6 32.4 %whole.1.both_ref = f32[4,4,4,128]{3,2,1,0:T(4,128)} custom-call(f32[3,4,4,128]{3,2,1,0:T(4,128)} %pos_hbm.1, f32[4,4,128]{2,1,0:T(4,128)} %chg_hbm.1, s32[4,4,4]{2,1,0:T(4,128)} %cnt_hbm.1, bf16[81,8,81]{2,1,0:T(8,128)(2,1)} %bitcast.2, bf16[81,8,81]{2,1,0:T(8,128)(2,1)} %bitcast.3, bf16[81,384]{1,0:T(8,128)(2,1)} %constant.6.slope_hbm, ...), custom_call_target="tpu_custom_call" | custom-call | tf_op jit(solution)/shard_map/whole/pallas_call | solution.py:676
  33.1 1.4 %part.1 = (f32[4,4,128]{2,1,0:T(4,128)}, f32[3,4,4,128]{3,2,1,0:T(4,128)}) custom-call(f32[4,4,4,128]{3,2,1,0:T(4,128)} %whole.1.both_ref), custom_call_target="tpu_custom_call" | custom-call | tf_op jit(solution)/shard_map/part/pallas_call | solution.py:732

commit v5 on v4

--- a/solution.py
+++ b/solution.py
@@ -15,7 +15,7 @@
 KPAD = 96
 LANES = 128
 OFFSETS = 316
-CHUNK = 4
+CHUNK = 2
 PIECES = 4
 MESH = pl.DeviceIdType.MESH
 F32 = jnp.float32
@@ -47,15 +47,9 @@
     return ((around[0] * 3 + around[1]) * 3 + around[2]) * 8 + inner[0] * 4 + inner[1] * 2 + inner[2]
 
 
-def offset_groups():
-    groups = {}
-    for index, shift in enumerate(offset_table()):
-        groups.setdefault(tuple(p for p, _ in admitted(shift)), []).append(index)
-    return sorted(groups.items(), key=lambda item: -len(item[0]))
-
-
 TOP_ROWS = {0: 10, 7: 11, 3: 12, 4: 13, 1: 14, 6: 15}
 EXTRA_TILES = {2: 216, 5: 217}
+TRIPLES = 106
 
 
 def top_parity(shift):
@@ -74,6 +68,17 @@
             for power_x in range(accumulated - height + 1):
                 listed.append((power_x, accumulated - height - power_x, height))
     return listed
+
+
+def triple_groups():
+    shifts = offset_table()
+    groups = {}
+    for triple in range(TRIPLES):
+        members = shifts[3 * triple : 3 * triple + 3]
+        parities = tuple(sorted({parity for shift in members for parity, _ in admitted(shift)}))
+        extra = [EXTRA_TILES[admitted(shift)[0][0]] for shift in members if top_parity(shift) is None]
+        groups.setdefault((parities, bool(extra)), []).append(triple)
+    return sorted(groups.items(), key=lambda item: (-len(item[0][0]), item[0]))
 
 
 def slope_matrix():
@@ -323,18 +328,18 @@
 
 def align_operators(first, last, whole_ref, aligned_ref):
     slots = {}
-    for _, members in offset_groups():
-        for index in members:
-            slots[index] = len(slots)
-    for index in range(first, last):
-        begin = index * TERMS
-        if begin + LANES <= whole_ref.shape[1]:
-            piece = whole_ref[:, begin : begin + LANES]
+    for _, members in triple_groups():
+        for triple in members:
+            slots[triple] = len(slots)
+    for triple in range(first, last):
+        begin = triple * 3 * TERMS
+        if begin + 256 <= whole_ref.shape[1]:
+            piece = whole_ref[:, begin : begin + 256]
         else:
-            tail = whole_ref[:, begin : begin + TERMS]
-            piece = jnp.concatenate([tail, jnp.zeros((TERMS, LANES - TERMS), BF16)], axis=1)
-        slot = slots[index]
-        aligned_ref[:TERMS, slot * LANES : (slot + 1) * LANES] = piece
+            tail = whole_ref[:, begin : OFFSETS * TERMS]
+            piece = jnp.concatenate([tail, jnp.zeros((TERMS, 256 - tail.shape[1]), BF16)], axis=1)
+        slot = slots[triple]
+        aligned_ref[:TERMS, slot * 256 : (slot + 1) * 256] = piece
 
 
 def clear_rows(rows_ref):
@@ -368,8 +373,15 @@
 
 
 def convert_tiles(rows_ref, tiles_ref):
+    lane = lax.broadcasted_iota(jnp.int32, (16, LANES), 1)
+    zero = jnp.zeros((16, LANES), BF16)
     for tile in range(218):
-        tiles_ref[tile] = rows_ref[tile * 16 : tile * 16 + 16, :].astype(BF16)
+        value = rows_ref[tile * 16 : tile * 16 + 16, :].astype(BF16)
+        second = pltpu.roll(value, TERMS, 1)
+        tiles_ref[0, tile] = value
+        tiles_ref[1, tile] = jnp.where(lane >= TERMS, second, zero)
+        tiles_ref[2, tile] = jnp.where(lane < TERMS, second, zero)
+        tiles_ref[3, tile] = pltpu.roll(value, 2 * TERMS - LANES, 1)
 
 
 def gather_top(tops, tops_ref, upper_ref, operators, lattice_ref, turned_ref, rows_ref):
@@ -398,13 +410,10 @@
             target = tile_of(place) * 16 + TOP_ROWS[parity]
             rows_ref[target : target + 1, :] = turned_ref[source : source + 1, :]
         else:
-            ((parity, place),) = admitted(shift)
-            begin, target = tile_of(place) * 16, EXTRA_TILES[parity] * 16
-            which = lax.broadcasted_iota(jnp.int32, (8, LANES), 0)
-            lower = jnp.where(which < 2, rows_ref[begin + 8 : begin + 16, :], 0.0)
-            top = jnp.broadcast_to(turned_ref[source : source + 1, :], (8, LANES))
-            rows_ref[target : target + 8, :] = rows_ref[begin : begin + 8, :]
-            rows_ref[target + 8 : target + 16, :] = jnp.where(which == 2, top, lower)
+            target = EXTRA_TILES[admitted(shift)[0][0]] * 16
+            which = lax.broadcasted_iota(jnp.int32, (16, LANES), 0)
+            top = jnp.broadcast_to(turned_ref[source : source + 1, :], (16, LANES))
+            rows_ref[target : target + 16, :] = jnp.where(which == 0, top, 0.0)
     return lattice_term
 
 
@@ -412,22 +421,40 @@
     total = [jnp.zeros((16, TERMS), F32) for _ in range(8)]
     extra = jnp.zeros((1, TERMS), F32)
     shifts = offset_table()
+    empty = jnp.zeros((16, LANES), BF16)
+
+    def lanes_of(sources):
+        halves_of = ([], [])
+        for position, tile in enumerate(sources):
+            if tile is not None:
+                for half, version in (((0, 0),), ((0, 1), (1, 2)), ((1, 3),))[position]:
+                    halves_of[half].append(tiles_ref[version, tile])
+        sides = [sum(side[1:], side[0]) if side else empty for side in halves_of]
+        return jnp.concatenate(sides, axis=1)
+
     slot = 0
-    for parities, members in offset_groups():
+    for (parities, special), members in triple_groups():
+        group = None
         for start in range(0, len(members), CHUNK):
             part = members[start : start + CHUNK]
-            special = len(parities) == 1 and parities[0] in EXTRA_TILES
             columns = []
-            for index in part:
-                tiles = [EXTRA_TILES[parities[0]]] if special else [tile_of(place) for _, place in admitted(shifts[index])]
-                columns.append(jnp.concatenate([tiles_ref[tile] for tile in tiles], axis=0))
+            for triple in part:
+                steps = shifts[3 * triple : 3 * triple + 3]
+                places = [dict(admitted(step)) for step in steps]
+                rows = [[tile_of(place[p]) if p in place else None for place in places] for p in parities]
+                if special:
+                    rows.append(
+                        [EXTRA_TILES[admitted(step)[0][0]] if top_parity(step) is None else None for step in steps]
+                    )
+                columns.append(jnp.concatenate([lanes_of(sources) for sources in rows], axis=0))
             data = columns[0] if len(columns) == 1 else jnp.concatenate(columns, axis=1)
-            product = lanes_nt(data, aligned_ref[:TERMS, slot * LANES : (slot + len(part)) * LANES])
+            product = lanes_nt(data, aligned_ref[:TERMS, slot * 256 : (slot + len(part)) * 256])
             slot += len(part)
-            for place, parity in enumerate(parities):
-                total[parity] = total[parity] + product[place * 16 : place * 16 + 16]
-            if special:
-                extra = extra + product[10:11]
+            group = product if group is None else group + product
+        for place, parity in enumerate(parities):
+            total[parity] = total[parity] + group[place * 16 : place * 16 + 16]
+        if special:
+            extra = extra + group[len(parities) * 16 : len(parities) * 16 + 1]
     for parity in range(8):
         acc_ref[parity * 16 : parity * 16 + 16, :] = widen(total[parity])
     return extra
@@ -623,26 +650,22 @@
     octant_operators(down_ref, down_rows)
     down_operators(octant_own, down_rows, downs_ref)
     clear_rows(rows_ref)
-    done = 0
-    for k in range(PIECES):
-        pieces[k].wait()
-        ready = OFFSETS if k == PIECES - 1 else ((k + 1) * (25600 // PIECES) - LANES) // TERMS
-        align_operators(done, ready, whole_ref, aligned_ref)
-        done = ready
     for copy in local:
         copy.wait()
     for index in order[:2]:
         halo[index].wait()
     inside = [(x, y) for x in range(1, 5) for y in range(1, 5)]
     fill_cells(inside, ext_ref, turned_ref, table_ref)
-    near_inside((0, 1), data_ref, table_ref, sums_ref)
+    near_inside((0, 1, 2, 3), data_ref, table_ref, sums_ref)
     for copy in first:
         copy.wait()
     second = [
         remote(tops_ref.at[ix], tops_ref.at[ix], gsend.at[32 + k], grecv.at[32 + k], step)
         for k, step in enumerate(line)
     ]
-    near_inside((2, 3), data_ref, table_ref, sums_ref)
+    for copy in pieces:
+        copy.wait()
+    align_operators(0, TRIPLES, whole_ref, aligned_ref)
     for index in order[2:]:
         halo[index].wait()
     fill_cells(
@@ -704,9 +727,9 @@
             pltpu.VMEM((6, 6, 3, 4, SLOTS, LANES), F32),
             pltpu.VMEM((4, 4, 4, 8, LANES), F32),
             pltpu.VMEM((TERMS, 25600), BF16),
-            pltpu.VMEM((KPAD, OFFSETS * LANES), BF16),
+            pltpu.VMEM((KPAD, TRIPLES * 256), BF16),
             pltpu.VMEM((218 * 16, LANES), F32),
-            pltpu.VMEM((218, 16, LANES), BF16),
+            pltpu.VMEM((4, 218, 16, LANES), BF16),
             pltpu.VMEM((8, 32, LANES), F32),
             pltpu.VMEM((32, LANES), F32),
             pltpu.VMEM((LANES, LANES), F32),

time: 34.6 us -> 34.2 us (0.988)
  Pallas kernels: 33.8 us -> 33.4 us
    pallas_call x1, Pallas kernels: 32.4 us -> 32 us  [whole_call(): pl.pallas_call(functools.partial(whole_kernel, *sizes), out_shape=shape(4...]
where the time goes in v5:
time: 34.2 us; the launch traced here: 34.1 us
  Pallas kernels  33.4 us (98%)
  between operations  0.64 us (2%)
    pallas_call x1, Pallas kernels, whole_call(): pl.pallas_call(functools.partial(whole_kernel, *sizes), out_shape=shape(4...  32 us
    pallas_call x1, Pallas kernels, part_call(): pl.pallas_call(part_kernel, out_shape=(shape(4, 4, LANES), shape(3, 4, 4,...  1.37 us

profile of v5, /device:TPU:1, one launch (start us, length us, event | category | flops | bytes accessed | tf_op | source)
XLA Modules:
  0.0 34.1 jit_solution(10334293223431332944)
XLA Ops:
  0.6 32.0 %whole.1.both_ref = f32[4,4,4,128]{3,2,1,0:T(4,128)} custom-call(f32[3,4,4,128]{3,2,1,0:T(4,128)} %pos_hbm.1, f32[4,4,128]{2,1,0:T(4,128)} %chg_hbm.1, s32[4,4,4]{2,1,0:T(4,128)} %cnt_hbm.1, bf16[81,8,81]{2,1,0:T(8,128)(2,1)} %bitcast.2, bf16[81,8,81]{2,1,0:T(8,128)(2,1)} %bitcast.3, bf16[81,384]{1,0:T(8,128)(2,1)} %constant.6.slope_hbm, ...), custom_call_target="tpu_custom_call" | custom-call | tf_op jit(solution)/shard_map/whole/pallas_call | solution.py:699
  32.7 1.4 %part.1 = (f32[4,4,128]{2,1,0:T(4,128)}, f32[3,4,4,128]{3,2,1,0:T(4,128)}) custom-call(f32[4,4,4,128]{3,2,1,0:T(4,128)} %whole.1.both_ref), custom_call_target="tpu_custom_call" | custom-call | tf_op jit(solution)/shard_map/part/pallas_call | solution.py:755

commit v6 on v5

--- a/solution.py
+++ b/solution.py
@@ -324,6 +324,16 @@
                     )
             for c in range(4):
                 sums_ref[x, y, c] = sums[c]
+
+
+def near_rows(sums_ref, data_ref, near_ref):
+    self_weight = lax.rsqrt(jnp.full((1, LANES), SOFTENING, F32))
+    for x in range(4):
+        for y in range(4):
+            near = [jnp.sum(sums_ref[x, y, c], axis=0, keepdims=True) for c in range(4)]
+            near[0] = near[0] - data_ref[x, y, 3:4, :] * self_weight
+            for c in range(4):
+                near_ref[c, x, y : y + 1, :] = near[c]
 
 
 def align_operators(first, last, whole_ref, aligned_ref):
@@ -488,7 +498,7 @@
         local_ref[octant * 8 : octant * 8 + 8, :] = widen(local)
 
 
-def evaluate(local_ref, slope_ref, high_ref, low_ref, sums_ref, data_ref, live_ref, out_ref):
+def evaluate(local_ref, slope_ref, high_ref, low_ref, near_ref, live_ref, out_ref):
     local_leaf = local_ref[...]
     upper, lower = halves(local_leaf[:, :TERMS])
     slopes = jnp.dot(upper, slope_ref[...], preferred_element_type=F32) + jnp.dot(
@@ -498,7 +508,6 @@
     split_parts = [halves(part[:, :KPAD]) for part in parts]
     row = lax.broadcasted_iota(jnp.int32, (16, LANES), 0)
     lane = lax.broadcasted_iota(jnp.int32, (16, LANES), 1)
-    self_weight = lax.rsqrt(jnp.full((1, LANES), SOFTENING, F32))
     for parity in range(4):
         span = slice(parity * 16, parity * 16 + 16)
         coef_high = jnp.concatenate([part[0][span] for part in split_parts], axis=0)
@@ -514,11 +523,10 @@
             sums = [
                 jnp.sum(jnp.where(hit, value[16 * c : 16 * c + 16], 0.0), axis=0, keepdims=True) for c in range(4)
             ]
-            near = [jnp.sum(sums_ref[x, y, c], axis=0, keepdims=True) for c in range(4)]
             live = live_ref[x, y : y + 1, :]
-            near[0] = near[0] - data_ref[x, y, 3:4, :] * self_weight
             for c in range(4):
-                value = near[c] + sums[c] if c == 0 else near[c] - sums[c]
+                near = near_ref[c, x, y : y + 1, :]
+                value = near + sums[c] if c == 0 else near - sums[c]
                 out_ref[c, x, y : y + 1, :] = value * live
 
 
@@ -559,6 +567,7 @@
     turned_ref,
     table_ref,
     sums_ref,
+    near_ref,
     whole_ref,
     aligned_ref,
     rows_ref,
@@ -587,9 +596,6 @@
     line = [(a, 0, 0) for a in range(1, nx)]
     wrapped = lambda step: (step[0] % nx, step[1] % ny, step[2] % nz)
     partners = sorted({wrapped(step) for step in DIRECTIONS} | set(plane) | set(line))
-    barrier = pltpu.get_barrier_semaphore()
-    for step in partners:
-        pl.semaphore_signal(barrier, inc=1, device_id=at(*step), device_id_type=MESH)
     operands = ((pos_hbm, pos_ref), (chg_hbm, chg_ref), (cnt_hbm, cnt_ref), (up_hbm, up_ref))
     operands += ((down_hbm, down_ref), (slope_hbm, slope_ref), (lattice_hbm, lattice_ref))
     loads = [pltpu.make_async_copy(src, dst, load.at[k]) for k, (src, dst) in enumerate(operands)]
@@ -597,7 +603,12 @@
     for k in range(PIECES):
         span = pl.ds(k * (25600 // PIECES), 25600 // PIECES)
         pieces.append(pltpu.make_async_copy(far_hbm.at[:, span], whole_ref.at[:, span], load.at[7 + k]))
-    for copy in loads + pieces:
+    for copy in loads[:4]:
+        copy.start()
+    barrier = pltpu.get_barrier_semaphore()
+    for step in partners:
+        pl.semaphore_signal(barrier, inc=1, device_id=at(*step), device_id_type=MESH)
+    for copy in pieces[:2] + loads[4:]:
         copy.start()
     octant_own = (ix % 2) * 4 + (iy % 2) * 2 + iz % 2
     for copy in loads[:4]:
@@ -606,7 +617,6 @@
     prepare(pos_ref, chg_ref, cnt_ref, data_ref, live_ref)
     octant_operators(up_ref, up_rows)
     monomial_tiles(rows_from(data_ref), high_ref, low_ref)
-    moments(data_ref, up_rows, leaf_ref, mid_ref, top_ref, high_ref, low_ref)
 
     pl.semaphore_wait(barrier, len(partners))
 
@@ -617,6 +627,17 @@
         copy.start()
         return copy
 
+    halo = {}
+    order = sorted(range(len(DIRECTIONS)), key=lambda i: sum(abs(d) for d in DIRECTIONS[i][:2]))
+    for index in order:
+        dx, dy, dz = DIRECTIONS[index]
+        from_x, to_x = span_of(dx, 4, 1)
+        from_y, to_y = span_of(dy, 4, 1)
+        src, dst = data_ref.at[from_x, from_y], ext_ref.at[to_x, to_y, 1 - dz]
+        halo[index] = remote(src, dst, send.at[0, index], recv.at[0, index], DIRECTIONS[index])
+    for copy in pieces[2:]:
+        copy.start()
+    moments(data_ref, up_rows, leaf_ref, mid_ref, top_ref, high_ref, low_ref)
     local = [
         pltpu.make_async_copy(data_ref, ext_ref.at[pl.ds(1, 4), pl.ds(1, 4), 1], own.at[0]),
         pltpu.make_async_copy(leaf_ref, wide_ref.at[pl.ds(1, 2), pl.ds(1, 2), pl.ds(1, 2)], own.at[1]),
@@ -625,14 +646,6 @@
     ]
     for copy in local:
         copy.start()
-    halo = {}
-    order = sorted(range(len(DIRECTIONS)), key=lambda i: sum(abs(d) for d in DIRECTIONS[i][:2]))
-    for index in order:
-        dx, dy, dz = DIRECTIONS[index]
-        from_x, to_x = span_of(dx, 4, 1)
-        from_y, to_y = span_of(dy, 4, 1)
-        src, dst = data_ref.at[from_x, from_y], ext_ref.at[to_x, to_y, 1 - dz]
-        halo[index] = remote(src, dst, send.at[0, index], recv.at[0, index], DIRECTIONS[index])
     first = [
         remote(top_ref, tops_ref.at[ix, iy, iz], gsend.at[k], grecv.at[k], step) for k, step in enumerate(plane)
     ]
@@ -645,11 +658,13 @@
         slot = ((1 - step[0]) * 3 + (1 - step[1])) * 3 + (1 - step[2])
         boxes.append(remote(mid_ref, mids_ref.at[slot], send.at[2, index], recv.at[2, index], step))
 
-    for copy in loads[4:]:
-        copy.wait()
-    octant_operators(down_ref, down_rows)
-    down_operators(octant_own, down_rows, downs_ref)
     clear_rows(rows_ref)
+    done = 0
+    for k in range(PIECES - 1):
+        pieces[k].wait()
+        ready = ((k + 1) * (25600 // PIECES) - 256) // (3 * TERMS)
+        align_operators(done, ready, whole_ref, aligned_ref)
+        done = ready
     for copy in local:
         copy.wait()
     for index in order[:2]:
@@ -663,15 +678,19 @@
         remote(tops_ref.at[ix], tops_ref.at[ix], gsend.at[32 + k], grecv.at[32 + k], step)
         for k, step in enumerate(line)
     ]
-    for copy in pieces:
+    pieces[-1].wait()
+    align_operators(done, TRIPLES, whole_ref, aligned_ref)
+    for copy in loads[4:]:
         copy.wait()
-    align_operators(0, TRIPLES, whole_ref, aligned_ref)
+    octant_operators(down_ref, down_rows)
+    down_operators(octant_own, down_rows, downs_ref)
     for index in order[2:]:
         halo[index].wait()
     fill_cells(
         [(x, y) for x in range(6) for y in range(6) if (x, y) not in inside], ext_ref, turned_ref, table_ref
     )
     near_outside(data_ref, table_ref, sums_ref)
+    near_rows(sums_ref, data_ref, near_ref)
     for copy in boxes:
         copy.wait()
     gather_boxes(wide_ref, mids_ref, rows_ref)
@@ -684,7 +703,7 @@
     convert_tiles(rows_ref, tiles_ref)
     extra = far_products(tiles_ref, aligned_ref, acc_ref)
     locals_down(octant_own, acc_ref, lattice_term + extra, downs_ref, local_ref)
-    evaluate(local_ref, slope_ref, high_ref, low_ref, sums_ref, data_ref, live_ref, out_ref)
+    evaluate(local_ref, slope_ref, high_ref, low_ref, near_ref, live_ref, out_ref)
 
 
 VMEM = pl.BlockSpec(memory_space=pltpu.VMEM)
@@ -726,6 +745,7 @@
             pltpu.VMEM((6, 6, 3, 4, LANES), F32),
             pltpu.VMEM((6, 6, 3, 4, SLOTS, LANES), F32),
             pltpu.VMEM((4, 4, 4, 8, LANES), F32),
+            pltpu.VMEM((4, 4, 4, LANES), F32),
             pltpu.VMEM((TERMS, 25600), BF16),
             pltpu.VMEM((KPAD, TRIPLES * 256), BF16),
             pltpu.VMEM((218 * 16, LANES), F32),

time: 34.2 us -> 34.4 us (level)
  no operation moved by 1% of the time
where the time goes in v6:
time: 34.4 us; the launch traced here: 34.3 us
  Pallas kernels  33.6 us (98%)
  between operations  0.64 us (2%)
    pallas_call x1, Pallas kernels, whole_call(): pl.pallas_call(functools.partial(whole_kernel, *sizes), out_shape=shape(4...  32.3 us
    pallas_call x1, Pallas kernels, part_call(): pl.pallas_call(part_kernel, out_shape=(shape(4, 4, LANES), shape(3, 4, 4,...  1.37 us

profile of v6, /device:TPU:1, one launch (start us, length us, event | category | flops | bytes accessed | tf_op | source)
XLA Modules:
  0.0 34.3 jit_solution(13363948228805740196)
XLA Ops:
  0.6 32.3 %whole.1.both_ref = f32[4,4,4,128]{3,2,1,0:T(4,128)} custom-call(f32[3,4,4,128]{3,2,1,0:T(4,128)} %pos_hbm.1, f32[4,4,128]{2,1,0:T(4,128)} %chg_hbm.1, s32[4,4,4]{2,1,0:T(4,128)} %cnt_hbm.1, bf16[81,8,81]{2,1,0:T(8,128)(2,1)} %bitcast.2, bf16[81,8,81]{2,1,0:T(8,128)(2,1)} %bitcast.3, bf16[81,384]{1,0:T(8,128)(2,1)} %constant.6.slope_hbm, ...), custom_call_target="tpu_custom_call" | custom-call | tf_op jit(solution)/shard_map/whole/pallas_call | solution.py:718
  32.9 1.4 %part.1 = (f32[4,4,128]{2,1,0:T(4,128)}, f32[3,4,4,128]{3,2,1,0:T(4,128)}) custom-call(f32[4,4,4,128]{3,2,1,0:T(4,128)} %whole.1.both_ref), custom_call_target="tpu_custom_call" | custom-call | tf_op jit(solution)/shard_map/part/pallas_call | solution.py:775

commit v7 on v6

--- a/solution.py
+++ b/solution.py
@@ -576,11 +576,10 @@
     coarse_ref,
     acc_ref,
     local_ref,
+    pool_ref,
+    line_ref,
     send,
     recv,
-    gsend,
-    grecv,
-    own,
     load,
 ):
     ix, iy, iz = lax.axis_index("gx"), lax.axis_index("gy"), lax.axis_index("gz")
@@ -627,36 +626,32 @@
         copy.start()
         return copy
 
-    halo = {}
     order = sorted(range(len(DIRECTIONS)), key=lambda i: sum(abs(d) for d in DIRECTIONS[i][:2]))
-    for index in order:
+    for rank, index in enumerate(order):
         dx, dy, dz = DIRECTIONS[index]
         from_x, to_x = span_of(dx, 4, 1)
         from_y, to_y = span_of(dy, 4, 1)
         src, dst = data_ref.at[from_x, from_y], ext_ref.at[to_x, to_y, 1 - dz]
-        halo[index] = remote(src, dst, send.at[0, index], recv.at[0, index], DIRECTIONS[index])
+        remote(src, dst, send.at[0], recv.at[0 if rank < 2 else 1], DIRECTIONS[index])
     for copy in pieces[2:]:
         copy.start()
     moments(data_ref, up_rows, leaf_ref, mid_ref, top_ref, high_ref, low_ref)
-    local = [
-        pltpu.make_async_copy(data_ref, ext_ref.at[pl.ds(1, 4), pl.ds(1, 4), 1], own.at[0]),
-        pltpu.make_async_copy(leaf_ref, wide_ref.at[pl.ds(1, 2), pl.ds(1, 2), pl.ds(1, 2)], own.at[1]),
-        pltpu.make_async_copy(mid_ref, mids_ref.at[13], own.at[2]),
-        pltpu.make_async_copy(top_ref, tops_ref.at[ix, iy, iz], own.at[3]),
-    ]
-    for copy in local:
-        copy.start()
-    first = [
-        remote(top_ref, tops_ref.at[ix, iy, iz], gsend.at[k], grecv.at[k], step) for k, step in enumerate(plane)
-    ]
-    boxes = []
-    for index, step in enumerate(DIRECTIONS):
+    pltpu.make_async_copy(data_ref, ext_ref.at[pl.ds(1, 4), pl.ds(1, 4), 1], recv.at[0]).start()
+    pltpu.make_async_copy(top_ref, tops_ref.at[ix, iy, iz], recv.at[2]).start()
+    pltpu.make_async_copy(leaf_ref, wide_ref.at[pl.ds(1, 2), pl.ds(1, 2), pl.ds(1, 2)], recv.at[4]).start()
+    pltpu.make_async_copy(mid_ref, mids_ref.at[13], recv.at[4]).start()
+    for step in plane:
+        remote(top_ref, tops_ref.at[ix, iy, iz], send.at[1], recv.at[2], step)
+    for step in DIRECTIONS:
         spans = [span_of(d, 2, 1) for d in step]
         src = leaf_ref.at[spans[0][0], spans[1][0], spans[2][0]]
         dst = wide_ref.at[spans[0][1], spans[1][1], spans[2][1]]
-        boxes.append(remote(src, dst, send.at[1, index], recv.at[1, index], step))
+        remote(src, dst, send.at[0], recv.at[4], step)
         slot = ((1 - step[0]) * 3 + (1 - step[1])) * 3 + (1 - step[2])
-        boxes.append(remote(mid_ref, mids_ref.at[slot], send.at[2, index], recv.at[2, index], step))
+        remote(mid_ref, mids_ref.at[slot], send.at[0], recv.at[4], step)
+
+    def drain(view, semaphore):
+        pltpu.make_async_copy(view, view, semaphore).wait()
 
     clear_rows(rows_ref)
     done = 0
@@ -665,37 +660,28 @@
         ready = ((k + 1) * (25600 // PIECES) - 256) // (3 * TERMS)
         align_operators(done, ready, whole_ref, aligned_ref)
         done = ready
-    for copy in local:
-        copy.wait()
-    for index in order[:2]:
-        halo[index].wait()
+    drain(ext_ref.at[pl.ds(0, 4), pl.ds(0, 4), pl.ds(0, 3)], recv.at[0])
     inside = [(x, y) for x in range(1, 5) for y in range(1, 5)]
     fill_cells(inside, ext_ref, turned_ref, table_ref)
     near_inside((0, 1, 2, 3), data_ref, table_ref, sums_ref)
-    for copy in first:
-        copy.wait()
-    second = [
-        remote(tops_ref.at[ix], tops_ref.at[ix], gsend.at[32 + k], grecv.at[32 + k], step)
-        for k, step in enumerate(line)
-    ]
+    drain(tops_ref.at[ix], recv.at[2])
+    for step in line:
+        remote(tops_ref.at[ix], tops_ref.at[ix], send.at[0], recv.at[3], step)
     pieces[-1].wait()
     align_operators(done, TRIPLES, whole_ref, aligned_ref)
     for copy in loads[4:]:
         copy.wait()
     octant_operators(down_ref, down_rows)
     down_operators(octant_own, down_rows, downs_ref)
-    for index in order[2:]:
-        halo[index].wait()
+    drain(ext_ref.at[pl.ds(0, 5), pl.ds(0, 4)], recv.at[1])
     fill_cells(
         [(x, y) for x in range(6) for y in range(6) if (x, y) not in inside], ext_ref, turned_ref, table_ref
     )
     near_outside(data_ref, table_ref, sums_ref)
     near_rows(sums_ref, data_ref, near_ref)
-    for copy in boxes:
-        copy.wait()
+    drain(pool_ref.at[pl.ds(0, 728)], recv.at[4])
     gather_boxes(wide_ref, mids_ref, rows_ref)
-    for copy in second:
-        copy.wait()
+    drain(tops_ref.at[pl.ds(0, 7)], recv.at[3])
     tops = (ix // 2, iy // 2, iz // 2)
     gather_upper(tops, tops_ref, rows_ref)
     operators = [octant_operator(up_rows, octant) for octant in range(8)]
@@ -704,6 +690,8 @@
     extra = far_products(tiles_ref, aligned_ref, acc_ref)
     locals_down(octant_own, acc_ref, lattice_term + extra, downs_ref, local_ref)
     evaluate(local_ref, slope_ref, high_ref, low_ref, near_ref, live_ref, out_ref)
+    drain(pool_ref, send.at[0])
+    drain(line_ref, send.at[1])
 
 
 VMEM = pl.BlockSpec(memory_space=pltpu.VMEM)
@@ -754,11 +742,10 @@
             pltpu.VMEM((32, LANES), F32),
             pltpu.VMEM((LANES, LANES), F32),
             pltpu.VMEM((64, LANES), F32),
-            dma((3, 26)),
-            dma((3, 26)),
-            dma((40,)),
-            dma((40,)),
-            dma((4,)),
+            pltpu.VMEM((1248, LANES), F32),
+            pltpu.VMEM((31, 1, LANES), F32),
+            dma((2,)),
+            dma((5,)),
             dma((7 + PIECES,)),
         ],
         compiler_params=pltpu.CompilerParams(collective_id=0, has_side_effects=True),

time: 34.4 us -> 32.3 us (0.939)
  Pallas kernels: 33.6 us -> 31.5 us
    pallas_call x1, Pallas kernels: 32.3 us -> 30.1 us  [whole_call(): pl.pallas_call(functools.partial(whole_kernel, *sizes), out_shape=shape(4...]
where the time goes in v7:
time: 32.3 us; the launch traced here: 32.1 us
  Pallas kernels  31.5 us (98%)
  between operations  0.64 us (2%)
    pallas_call x1, Pallas kernels, whole_call(): pl.pallas_call(functools.partial(whole_kernel, *sizes), out_shape=shape(4...  30.1 us
    pallas_call x1, Pallas kernels, part_call(): pl.pallas_call(part_kernel, out_shape=(shape(4, 4, LANES), shape(3, 4, 4,...  1.37 us

profile of v7, /device:TPU:1, one launch (start us, length us, event | category | flops | bytes accessed | tf_op | source)
XLA Modules:
  0.0 32.1 jit_solution(10171774516386707538)
XLA Ops:
  0.6 30.1 %whole.1.both_ref = f32[4,4,4,128]{3,2,1,0:T(4,128)} custom-call(f32[3,4,4,128]{3,2,1,0:T(4,128)} %pos_hbm.1, f32[4,4,128]{2,1,0:T(4,128)} %chg_hbm.1, s32[4,4,4]{2,1,0:T(4,128)} %cnt_hbm.1, bf16[81,8,81]{2,1,0:T(8,128)(2,1)} %bitcast.2, bf16[81,8,81]{2,1,0:T(8,128)(2,1)} %bitcast.3, bf16[81,384]{1,0:T(8,128)(2,1)} %constant.6.slope_hbm, ...), custom_call_target="tpu_custom_call" | custom-call | tf_op jit(solution)/shard_map/whole/pallas_call | solution.py:706
  30.7 1.4 %part.1 = (f32[4,4,128]{2,1,0:T(4,128)}, f32[3,4,4,128]{3,2,1,0:T(4,128)}) custom-call(f32[4,4,4,128]{3,2,1,0:T(4,128)} %whole.1.both_ref), custom_call_target="tpu_custom_call" | custom-call | tf_op jit(solution)/shard_map/part/pallas_call | solution.py:762

commit v8 on v7

--- a/solution.py
+++ b/solution.py
@@ -224,13 +224,16 @@
     return pl.ds(0, 1), pl.ds(first + own, 1)
 
 
-def fill_cells(cells, ext_ref, turned_ref, table_ref):
+def turn_cells(cells, ext_ref, turned_ref):
     lane4 = lax.broadcasted_iota(jnp.int32, (4, LANES), 1)
     for x, y in cells:
         before, here, after = ext_ref[x, y, 0], ext_ref[x, y, 1], ext_ref[x, y, 2]
         turned_ref[x, y, 0] = pltpu.roll(jnp.where(lane4 >= 96, before, here), 32, 1)
         turned_ref[x, y, 1] = here
         turned_ref[x, y, 2] = pltpu.roll(jnp.where(lane4 < 32, after, here), 96, 1)
+
+
+def fill_cells(cells, shifts, rows_of, table_ref):
     lane = lax.broadcasted_iota(jnp.int32, (8, LANES), 1)
     base = lane // SLOTS * SLOTS + lax.broadcasted_iota(jnp.int32, (8, LANES), 0)
 
@@ -238,9 +241,10 @@
         pick = base + group * 8
         start = pl.multiple_of(group * 8, 8)
         for x, y in cells:
-            for ez in range(3):
+            for ez in shifts:
+                rows = rows_of(x, y, ez)
                 for c in range(4):
-                    row = jnp.broadcast_to(turned_ref[x, y, ez, c : c + 1, :], (8, LANES))
+                    row = jnp.broadcast_to(rows[c : c + 1, :], (8, LANES))
                     table_ref[x, y, ez, c, pl.ds(start, 8), :] = jnp.take_along_axis(row, pick, axis=1)
         return carry
 
@@ -607,7 +611,7 @@
     barrier = pltpu.get_barrier_semaphore()
     for step in partners:
         pl.semaphore_signal(barrier, inc=1, device_id=at(*step), device_id_type=MESH)
-    for copy in pieces[:2] + loads[4:]:
+    for copy in pieces + loads[4:]:
         copy.start()
     octant_own = (ix % 2) * 4 + (iy % 2) * 2 + iz % 2
     for copy in loads[:4]:
@@ -633,8 +637,6 @@
         from_y, to_y = span_of(dy, 4, 1)
         src, dst = data_ref.at[from_x, from_y], ext_ref.at[to_x, to_y, 1 - dz]
         remote(src, dst, send.at[0], recv.at[0 if rank < 2 else 1], DIRECTIONS[index])
-    for copy in pieces[2:]:
-        copy.start()
     moments(data_ref, up_rows, leaf_ref, mid_ref, top_ref, high_ref, low_ref)
     pltpu.make_async_copy(data_ref, ext_ref.at[pl.ds(1, 4), pl.ds(1, 4), 1], recv.at[0]).start()
     pltpu.make_async_copy(top_ref, tops_ref.at[ix, iy, iz], recv.at[2]).start()
@@ -655,28 +657,29 @@
 
     clear_rows(rows_ref)
     done = 0
-    for k in range(PIECES - 1):
+    inside = [(x, y) for x in range(1, 5) for y in range(1, 5)]
+    fill_cells(inside, (1,), lambda x, y, ez: data_ref.at[x - 1, y - 1], table_ref)
+    for copy in loads[4:]:
+        copy.wait()
+    octant_operators(down_ref, down_rows)
+    down_operators(octant_own, down_rows, downs_ref)
+    for k in range(PIECES):
         pieces[k].wait()
-        ready = ((k + 1) * (25600 // PIECES) - 256) // (3 * TERMS)
+        ready = TRIPLES if k == PIECES - 1 else ((k + 1) * (25600 // PIECES) - 256) // (3 * TERMS)
         align_operators(done, ready, whole_ref, aligned_ref)
         done = ready
     drain(ext_ref.at[pl.ds(0, 4), pl.ds(0, 4), pl.ds(0, 3)], recv.at[0])
-    inside = [(x, y) for x in range(1, 5) for y in range(1, 5)]
-    fill_cells(inside, ext_ref, turned_ref, table_ref)
+    turn_cells(inside, ext_ref, turned_ref)
+    turned = lambda x, y, ez: turned_ref.at[x, y, ez]
+    fill_cells(inside, (0, 2), turned, table_ref)
     near_inside((0, 1, 2, 3), data_ref, table_ref, sums_ref)
     drain(tops_ref.at[ix], recv.at[2])
     for step in line:
         remote(tops_ref.at[ix], tops_ref.at[ix], send.at[0], recv.at[3], step)
-    pieces[-1].wait()
-    align_operators(done, TRIPLES, whole_ref, aligned_ref)
-    for copy in loads[4:]:
-        copy.wait()
-    octant_operators(down_ref, down_rows)
-    down_operators(octant_own, down_rows, downs_ref)
     drain(ext_ref.at[pl.ds(0, 5), pl.ds(0, 4)], recv.at[1])
-    fill_cells(
-        [(x, y) for x in range(6) for y in range(6) if (x, y) not in inside], ext_ref, turned_ref, table_ref
-    )
+    outside = [(x, y) for x in range(6) for y in range(6) if (x, y) not in inside]
+    turn_cells(outside, ext_ref, turned_ref)
+    fill_cells(outside, (0, 1, 2), turned, table_ref)
     near_outside(data_ref, table_ref, sums_ref)
     near_rows(sums_ref, data_ref, near_ref)
     drain(pool_ref.at[pl.ds(0, 728)], recv.at[4])

time: 32.3 us -> 33.5 us (1.037)
  Pallas kernels: 31.5 us -> 32.7 us
    pallas_call x1, Pallas kernels: 30.1 us -> 31.3 us  [whole_call(): pl.pallas_call(functools.partial(whole_kernel, *sizes), out_shape=shape(4...]
where the time goes in v8:
time: 33.5 us; the launch traced here: 33.3 us
  Pallas kernels  32.7 us (98%)
  between operations  0.64 us (2%)
    pallas_call x1, Pallas kernels, whole_call(): pl.pallas_call(functools.partial(whole_kernel, *sizes), out_shape=shape(4...  31.3 us
    pallas_call x1, Pallas kernels, part_call(): pl.pallas_call(part_kernel, out_shape=(shape(4, 4, LANES), shape(3, 4, 4,...  1.37 us

profile of v8, /device:TPU:1, one launch (start us, length us, event | category | flops | bytes accessed | tf_op | source)
XLA Modules:
  0.0 33.3 jit_solution(5795068959013157775)
XLA Ops:
  0.6 31.3 %whole.1.both_ref = f32[4,4,4,128]{3,2,1,0:T(4,128)} custom-call(f32[3,4,4,128]{3,2,1,0:T(4,128)} %pos_hbm.1, f32[4,4,128]{2,1,0:T(4,128)} %chg_hbm.1, s32[4,4,4]{2,1,0:T(4,128)} %cnt_hbm.1, bf16[81,8,81]{2,1,0:T(8,128)(2,1)} %bitcast.2, bf16[81,8,81]{2,1,0:T(8,128)(2,1)} %bitcast.3, bf16[81,384]{1,0:T(8,128)(2,1)} %constant.6.slope_hbm, ...), custom_call_target="tpu_custom_call" | custom-call | tf_op jit(solution)/shard_map/whole/pallas_call | solution.py:709
  31.9 1.4 %part.1 = (f32[4,4,128]{2,1,0:T(4,128)}, f32[3,4,4,128]{3,2,1,0:T(4,128)}) custom-call(f32[4,4,4,128]{3,2,1,0:T(4,128)} %whole.1.both_ref), custom_call_target="tpu_custom_call" | custom-call | tf_op jit(solution)/shard_map/part/pallas_call | solution.py:765

commit v9 on v8

--- a/solution.py
+++ b/solution.py
@@ -611,7 +611,7 @@
     barrier = pltpu.get_barrier_semaphore()
     for step in partners:
         pl.semaphore_signal(barrier, inc=1, device_id=at(*step), device_id_type=MESH)
-    for copy in pieces + loads[4:]:
+    for copy in pieces[:2] + loads[4:]:
         copy.start()
     octant_own = (ix % 2) * 4 + (iy % 2) * 2 + iz % 2
     for copy in loads[:4]:
@@ -637,6 +637,8 @@
         from_y, to_y = span_of(dy, 4, 1)
         src, dst = data_ref.at[from_x, from_y], ext_ref.at[to_x, to_y, 1 - dz]
         remote(src, dst, send.at[0], recv.at[0 if rank < 2 else 1], DIRECTIONS[index])
+    for copy in pieces[2:]:
+        copy.start()
     moments(data_ref, up_rows, leaf_ref, mid_ref, top_ref, high_ref, low_ref)
     pltpu.make_async_copy(data_ref, ext_ref.at[pl.ds(1, 4), pl.ds(1, 4), 1], recv.at[0]).start()
     pltpu.make_async_copy(top_ref, tops_ref.at[ix, iy, iz], recv.at[2]).start()
@@ -659,13 +661,9 @@
     done = 0
     inside = [(x, y) for x in range(1, 5) for y in range(1, 5)]
     fill_cells(inside, (1,), lambda x, y, ez: data_ref.at[x - 1, y - 1], table_ref)
-    for copy in loads[4:]:
-        copy.wait()
-    octant_operators(down_ref, down_rows)
-    down_operators(octant_own, down_rows, downs_ref)
-    for k in range(PIECES):
+    for k in range(PIECES - 1):
         pieces[k].wait()
-        ready = TRIPLES if k == PIECES - 1 else ((k + 1) * (25600 // PIECES) - 256) // (3 * TERMS)
+        ready = ((k + 1) * (25600 // PIECES) - 256) // (3 * TERMS)
         align_operators(done, ready, whole_ref, aligned_ref)
         done = ready
     drain(ext_ref.at[pl.ds(0, 4), pl.ds(0, 4), pl.ds(0, 3)], recv.at[0])
@@ -676,6 +674,12 @@
     drain(tops_ref.at[ix], recv.at[2])
     for step in line:
         remote(tops_ref.at[ix], tops_ref.at[ix], send.at[0], recv.at[3], step)
+    pieces[-1].wait()
+    align_operators(done, TRIPLES, whole_ref, aligned_ref)
+    for copy in loads[4:]:
+        copy.wait()
+    octant_operators(down_ref, down_rows)
+    down_operators(octant_own, down_rows, downs_ref)
     drain(ext_ref.at[pl.ds(0, 5), pl.ds(0, 4)], recv.at[1])
     outside = [(x, y) for x in range(6) for y in range(6) if (x, y) not in inside]
     turn_cells(outside, ext_ref, turned_ref)

time: 33.5 us -> 32.6 us (0.973)
  Pallas kernels: 32.7 us -> 31.8 us
    pallas_call x1, Pallas kernels: 31.3 us -> 30.4 us  [whole_call(): pl.pallas_call(functools.partial(whole_kernel, *sizes), out_shape=shape(4...]
where the time goes in v9:
time: 32.6 us; the launch traced here: 32.4 us
  Pallas kernels  31.8 us (98%)
  between operations  0.64 us (2%)
    pallas_call x1, Pallas kernels, whole_call(): pl.pallas_call(functools.partial(whole_kernel, *sizes), out_shape=shape(4...  30.4 us
    pallas_call x1, Pallas kernels, part_call(): pl.pallas_call(part_kernel, out_shape=(shape(4, 4, LANES), shape(3, 4, 4,...  1.37 us

profile of v9, /device:TPU:1, one launch (start us, length us, event | category | flops | bytes accessed | tf_op | source)
XLA Modules:
  0.0 32.4 jit_solution(14178296517195282796)
XLA Ops:
  0.6 30.4 %whole.1.both_ref = f32[4,4,4,128]{3,2,1,0:T(4,128)} custom-call(f32[3,4,4,128]{3,2,1,0:T(4,128)} %pos_hbm.1, f32[4,4,128]{2,1,0:T(4,128)} %chg_hbm.1, s32[4,4,4]{2,1,0:T(4,128)} %cnt_hbm.1, bf16[81,8,81]{2,1,0:T(8,128)(2,1)} %bitcast.2, bf16[81,8,81]{2,1,0:T(8,128)(2,1)} %bitcast.3, bf16[81,384]{1,0:T(8,128)(2,1)} %constant.6.slope_hbm, ...), custom_call_target="tpu_custom_call" | custom-call | tf_op jit(solution)/shard_map/whole/pallas_call | solution.py:713
  31.0 1.4 %part.1 = (f32[4,4,128]{2,1,0:T(4,128)}, f32[3,4,4,128]{3,2,1,0:T(4,128)}) custom-call(f32[4,4,4,128]{3,2,1,0:T(4,128)} %whole.1.both_ref), custom_call_target="tpu_custom_call" | custom-call | tf_op jit(solution)/shard_map/part/pallas_call | solution.py:769
